TPU v7x, 32 devices: a 4x4x1 block of a 4x4x8 slice. The times are simulated.
32 devices in a mesh: data: 1 (over z), outer: 4 (over y), expert: 8 (over x, core).
Axes of the slice: x: 4, y: 4, z: 1, core: 2. Of those that a mesh axis runs over, the one named last changes fastest.
The devices are a block of a 4x4x8 slice.
Arguments:
- x: bfloat16 [16384, 2048], P(('data', 'outer', 'expert'))
- wr: bfloat16 [2048, 128], replicated
- idx: int32 [16384, 8], P(('data', 'outer', 'expert'))
- w1: bfloat16 [128, 2048, 768], P(('outer', 'expert'))
- w3: bfloat16 [128, 2048, 768], P(('outer', 'expert'))
- w2: bfloat16 [128, 768, 2048], P(('outer', 'expert'))
Outputs:
- output: bfloat16 [16384, 2048], P(('data', 'outer', 'expert'))
All inputs are finite; a program needn't handle non-finite values.
Results may differ from a plain program's by a relative error of at most 0.0081153.
Values are sent between devices in bfloat16 or wider.
A program may use at most 768 MiB of HBM per device.

v0:
```python
import jax
import jax.numpy as jnp
from jax import lax
from jax.sharding import PartitionSpec as P


def _gate(x, wr, idx):
    logits = jnp.dot(x, wr, preferred_element_type=jnp.float32)
    oh = idx[:, :, None] == jnp.arange(wr.shape[1], dtype=idx.dtype)
    return jax.nn.softmax(jnp.sum(jnp.where(oh, logits[:, None, :], 0.0), axis=-1), axis=-1)


def _plan(idx, g, base, ne, cap):
    t = idx.shape[-2]
    oh = idx[..., None] == base + jnp.arange(ne, dtype=idx.dtype)
    m = jnp.sum(oh, axis=-2, dtype=jnp.int32).astype(jnp.float32)
    pos = jnp.arange(t, dtype=jnp.int32)
    tri = (pos[None, :] < pos[:, None]).astype(jnp.bfloat16)
    cnt = jnp.einsum('uv,...ve->...ue', tri, m.astype(jnp.bfloat16), preferred_element_type=jnp.float32)
    c = jnp.arange(cap, dtype=jnp.float32)
    hit = (c >= cnt[..., None]) & (c < (cnt + m)[..., None])
    ge = jnp.sum(jnp.where(oh, g[..., None], 0.0), axis=-2)
    w = jnp.where(hit, ge[..., None], 0.0)
    return hit.astype(jnp.bfloat16), w


def _split(w):
    hi = w.astype(jnp.bfloat16)
    r = w - hi.astype(jnp.float32)
    mid = r.astype(jnp.bfloat16)
    lo = (r - mid.astype(jnp.float32)).astype(jnp.bfloat16)
    return jnp.stack([hi, mid, lo])


def solution(mesh):
    O = mesh.shape['outer']
    X = mesh.shape['expert']
    n = O * X
    tok = P(('data', 'outer', 'expert'), None)
    wsp = P(('outer', 'expert'), None, None)

    def local(x, wr, idx, w1, w3, w2):
        T, dm = x.shape
        k = idx.shape[1]
        E = wr.shape[1]
        el = w1.shape[0]
        C = 2 * T * k // E
        g = _gate(x, wr, idx)
        hit, w = _plan(idx, g, 0, E, C)
        ws = _split(w).reshape(3 * T, E * C)
        buf = jnp.einsum('tec,td->ecd', hit, x, preferred_element_type=jnp.float32).astype(x.dtype)
        buf = buf.reshape(O, X, el * C, dm)
        buf = lax.all_to_all(buf, 'expert', 1, 1, tiled=True)
        buf = lax.all_to_all(buf, 'outer', 0, 0, tiled=True)
        xin = buf.reshape(n, el, C, dm).transpose(1, 0, 2, 3).reshape(el, n * C, dm)
        a = jnp.einsum('ecd,edf->ecf', xin, w1, preferred_element_type=jnp.float32)
        b = jnp.einsum('ecd,edf->ecf', xin, w3, preferred_element_type=jnp.float32)
        h = (jax.nn.silu(a) * b).astype(jnp.bfloat16)
        o = jnp.einsum('ecf,efd->ecd', h, w2, preferred_element_type=jnp.float32).astype(jnp.bfloat16)
        o = o.reshape(el, n, C, dm).transpose(1, 0, 2, 3).reshape(O, X, el * C, dm)
        o = lax.all_to_all(o, 'outer', 0, 0, tiled=True)
        o = lax.all_to_all(o, 'expert', 1, 1, tiled=True)
        y = jnp.dot(ws, o.reshape(E * C, dm), preferred_element_type=jnp.float32)
        return jnp.sum(y.reshape(3, T, dm), axis=0).astype(jnp.bfloat16)

    return jax.shard_map(local, mesh=mesh, in_specs=(tok, P(None, None), tok, wsp, wsp, wsp), out_specs=tok, check_vma=False)
```

profile of v0, /device:TPU:97, one launch (start us, length us, event | category | flops | bytes accessed | tf_op | source)
XLA Modules:
  0.0 1882.0 jit_solution(748952142624625289)
XLA Ops:
  7.9 24.6 %convolution_convert_fusion.1 = bf16[128,64,2048]{2,0,1:T(8,128)(2,1)} fusion(pred[512,128,64]{0,2,1:T(32,128)(4,1)S(1)} %fusion.6, bf16[512,2048]{1,0:T(8,128)(2,1)S(1)} %copy-done), kind=kOutput, calls=%fused_computation.8 | convolution fusion | flops 17196646400 | bytes 39845888 | tf_op jit(solution)/shard_map/tec,td->ecd/dot_general | solution.py:51
  32.5 30.0 %copy.66 = bf16[128,64,2048]{2,1,0:T(8,128)(2,1)} copy(bf16[128,64,2048]{2,0,1:T(8,128)(2,1)} %convolution_convert_fusion.1) | data formatting | bytes 67108864 | tf_op jit(solution)/shard_map/convert_element_type | solution.py:51
  62.5 23.0 %copy.67 = bf16[4,8,256,2048]{3,2,0,1:T(8,128)(2,1)} copy(bf16[4,8,256,2048]{3,2,1,0:T(8,128)(2,1)} %bitcast.35) | data formatting | bytes 67108864 | tf_op jit(solution)/shard_map/reshape | solution.py:52
  85.5 376.3 %all_to_all.20 = bf16[4,8,256,2048]{3,2,0,1:T(8,128)(2,1)} all-to-all(bf16[4,8,256,2048]{3,2,0,1:T(8,128)(2,1)} %copy.67), channel_id=1, replica_groups=mesh['data'=1,'outer'=4,'expert'=8] {'expert'}, dimensions={1} | all-to-all | bytes 67108864 | tf_op jit(solution)/shard_map/all_to_all | solution.py:53
  461.7 22.9 %copy.68 = bf16[4,8,256,2048]{3,2,1,0:T(8,128)(2,1)} copy(bf16[4,8,256,2048]{3,2,0,1:T(8,128)(2,1)} %all_to_all.20) | data formatting | bytes 67108864 | tf_op jit(solution)/shard_map/all_to_all | solution.py:53
  484.7 382.0 %all_to_all.21 = bf16[4,8,256,2048]{3,2,1,0:T(8,128)(2,1)} all-to-all(bf16[4,8,256,2048]{3,2,1,0:T(8,128)(2,1)} %copy.68), channel_id=1, replica_groups=mesh['data'=1,'outer'=4,'expert'=8] {'outer'}, dimensions={0} | all-to-all | bytes 67108864 | tf_op jit(solution)/shard_map/all_to_all | solution.py:54
  866.7 22.9 %copy.69 = bf16[4,32,64,2048]{3,2,1,0:T(8,128)(2,1)} copy(bf16[4,32,64,2048]{3,2,0,1:T(8,128)(2,1)} %bitcast.36) | data formatting | bytes 67108864 | tf_op jit(solution)/shard_map/transpose | solution.py:55
  889.6 36.2 %fusion.23 = f32[4,2048,768]{2,1,0:T(8,128)} fusion(bf16[4,2048,2048]{2,1,0:T(8,128)(2,1)} %bitcast.42, bf16[4,2048,768]{2,1,0:T(8,128)(2,1)} %param.9), kind=kOutput, calls=%fused_computation.36 | convolution fusion | flops 25769803776 | bytes 71303168 | tf_op jit(solution)/shard_map/ecd,edf->ecf/dot_general | solution.py:56
  925.8 38.2 %multiply_convert_fusion.4 = bf16[4,2048,768]{2,1,0:T(8,128)(2,1)} fusion(f32[4,2048,768]{2,1,0:T(8,128)} %fusion.23, bf16[4,2048,2048]{2,1,0:T(8,128)(2,1)} %bitcast.43, bf16[4,2048,768]{2,1,0:T(8,128)(2,1)} %param.10), kind=kOutput, calls=%fused_computation.7.clone.clone.1 | convolution fusion | flops 25807552512 | bytes 83886080 | tf_op jit(solution)/shard_map/ecd,edf->ecf/dot_general | solution.py:57
  964.0 35.8 %convolution_convert_fusion = bf16[4,2048,2048]{2,1,0:T(8,128)(2,1)} fusion(bf16[4,768,2048]{2,1,0:T(8,128)(2,1)} %param.11, bf16[4,2048,768]{2,1,0:T(8,128)(2,1)} %multiply_convert_fusion.4), kind=kOutput, calls=%fused_computation | convolution fusion | flops 25786580992 | bytes 58720256 | tf_op jit(solution)/shard_map/ecf,efd->ecd/dot_general | solution.py:59
  999.8 23.0 %copy.70 = bf16[4,32,64,2048]{3,2,0,1:T(8,128)(2,1)} copy(bf16[4,32,64,2048]{3,2,1,0:T(8,128)(2,1)} %bitcast.44) | data formatting | bytes 67108864 | tf_op jit(solution)/shard_map/reshape | solution.py:60
  1022.7 380.2 %all_to_all.22 = bf16[4,8,256,2048]{3,2,1,0:T(8,128)(2,1)} all-to-all(bf16[4,8,256,2048]{3,2,1,0:T(8,128)(2,1)} %bitcast.37), channel_id=1, replica_groups=mesh['data'=1,'outer'=4,'expert'=8] {'outer'}, dimensions={0} | all-to-all | bytes 67108864 | tf_op jit(solution)/shard_map/all_to_all | solution.py:61
  1403.0 22.9 %copy.71 = bf16[4,8,256,2048]{3,2,0,1:T(8,128)(2,1)} copy(bf16[4,8,256,2048]{3,2,1,0:T(8,128)(2,1)} %all_to_all.22) | data formatting | bytes 67108864 | tf_op jit(solution)/shard_map/all_to_all | solution.py:61
  1426.0 9.1 all-to-all-start.3
  1446.3 8.0 ge.52
  1454.3 17.5 copy.57
  1471.7 7.9 lt.49
  1479.6 17.4 copy.59
  1497.0 7.9 broadcast_in_dim.54
  1504.9 17.4 copy.64
  1522.3 20.6 %fusion.21 = (bf16[1,512,8192]{2,1,0:T(8,128)(2,1)}, f32[1,512,8192]{2,1,0:T(8,128)S(1)}) fusion(f32[1,512,8192]{2,1,0:T(8,128)} %copy.64, f32[1,512,8192]{2,1,0:T(8,128)} %copy.59, f32[1,512,8192]{2,1,0:T(8,128)} %copy.57, f32[8192]{0:T(1024)S(1)} %ge.50), kind=kLoop, calls=%fused_computation.34 | loop fusion | flops 20971520 | bytes 75530240 | tf_op jit(solution)/shard_map/convert_element_type | solution.py:28
  1549.7 248.7 %all-to-all-done.3 = bf16[4,8,256,2048]{3,2,0,1:T(8,128)(2,1)} async-done(((bf16[4,8,256,2048]{3,2,0,1:T(8,128)(2,1)}), bf16[4,8,256,2048]{3,2,0,1:T(8,128)(2,1)}, u32[]{:S(2)}, u32[]{:S(2)}) %all-to-all-start.3) | async-done | bytes 33554464 | tf_op jit(solution)/shard_map/all_to_all | solution.py:62
  1798.3 22.9 %copy.72 = bf16[4,8,256,2048]{3,2,1,0:T(8,128)(2,1)} copy(bf16[4,8,256,2048]{3,2,0,1:T(8,128)(2,1)} %all-to-all-done.3) | data formatting | bytes 67108864 | tf_op jit(solution)/shard_map/all_to_all | solution.py:62
  1821.3 60.3 %fusion.12 = bf16[512,2048]{1,0:T(8,128)(2,1)} fusion(bf16[8192,2048,1]{1,0,2:T(8,128)(2,1)} %bitcast.41, bf16[1,512,8192]{2,1,0:T(8,128)(2,1)} %get-tuple-element.8, bf16[1,512,8192]{2,1,0:T(8,128)(2,1)} %get-tuple-element.7, bf16[1,512,8192]{2,1,0:T(8,128)(2,1)} %get-tuple-element.5), kind=kOutput, calls=%fused_computation.19 | convolution fusion | flops 51566870528 | bytes 60817408 | tf_op jit(solution)/shard_map/dot_general | solution.py:63
  (34 shorter events, 25.7 us)
Async XLA Ops:
  0.0 7.9 copy-start
  1.0 31.5 %copy-start.1 = (s32[512,8]{1,0:T(8,128)}, s32[512,8]{1,0:T(8,128)S(1)}, u32[]{:S(2)}) copy-start(s32[512,8]{1,0:T(8,128)S(1)} %copy.55) | copy-start | bytes 49156
  4.3 28.2 %copy-start.3 = (f32[512,128]{0,1:T(8,128)}, f32[512,128]{0,1:T(8,128)S(1)}, u32[]{:S(2)}) copy-start(f32[512,128]{0,1:T(8,128)S(1)} %copy.58) | copy-start | bytes 786436
  4.5 28.0 %copy-start.5 = (f32[512,128]{0,1:T(8,128)}, f32[512,128]{0,1:T(8,128)S(1)}, u32[]{:S(2)}) copy-start(f32[512,128]{0,1:T(8,128)S(1)} %copy.56) | copy-start | bytes 786436
  1425.9 9.2 copy-start.7
  1425.9 10.0 copy-start.2
  1425.9 20.3 %copy-start.6 = (f32[512,128]{0,1:T(8,128)S(1)}, f32[512,128]{0,1:T(8,128)}, u32[]{:S(2)}) copy-start(f32[512,128]{0,1:T(8,128)} %copy-done.5) | copy-start | bytes 786436
  1426.0 372.4 %all-to-all-start.3 = ((bf16[4,8,256,2048]{3,2,0,1:T(8,128)(2,1)}), bf16[4,8,256,2048]{3,2,0,1:T(8,128)(2,1)}, u32[]{:S(2)}, u32[]{:S(2)}) async-start(bf16[4,8,256,2048]{3,2,0,1:T(8,128)(2,1)} %copy.71), calls=%async_computation.3 | async-start | bytes 67108864 | tf_op jit(solution)/shard_map/all_to_all | solution.py:62
  1454.2 17.5 copy-start.4
where the time goes:
time: 1900 us; the launch traced here: 1880 us
  blocking collectives  1140 us (60%)
  waiting for transfers between devices  249 us (13%)
  local copies, waits for them, and re-layouts  245 us (13%)
  matrix products  196 us (10%)
  other arithmetic  43.6 us (2%)
    all_to_all x1, blocking collectives, local(): buf = lax.all_to_all(buf, 'outer', 0, 0, tiled=True)  382 us
    all_to_all x1, blocking collectives, local(): o = lax.all_to_all(o, 'outer', 0, 0, tiled=True)  380 us
    all_to_all x1, blocking collectives, local(): buf = lax.all_to_all(buf, 'expert', 1, 1, tiled=True)  376 us
    all_to_all x1, waiting for transfers between devices, local(): o = lax.all_to_all(o, 'expert', 1, 1, tiled=True)  249 us
    dot_general x1, matrix products, local(): y = jnp.dot(ws, o.reshape(E * C, dm), preferred_element_type=jnp.float32)  60.3 us
    dot_general x1, matrix products, local(): b = jnp.einsum('ecd,edf->ecf', xin, w3, preferred_element_type=jnp.float32)  38.2 us
  transfers between devices with their start and end apart: 1, of which 1 were waited for; matrix products, arithmetic and copies ran while one was open for 6% of the time, Pallas kernels for 0%

commit v1 on v0

v1 whole, which is shorter than its diff:
```python
import functools

import jax
import jax.numpy as jnp
from jax import lax
from jax.experimental import pallas as pl
from jax.experimental.pallas import tpu as pltpu
from jax.sharding import PartitionSpec as P

MESH = pl.DeviceIdType.MESH
F32 = jnp.float32
BF16 = jnp.bfloat16


def _gate(x, wr, idx):
    logits = jnp.dot(x, wr, preferred_element_type=F32)
    oh = idx[:, :, None] == jnp.arange(wr.shape[1], dtype=idx.dtype)
    return jax.nn.softmax(jnp.sum(jnp.where(oh, logits[:, None, :], 0.0), axis=-1), axis=-1)


def _parts(w):
    hi = lax.reduce_precision(w, 8, 7)
    r = w - hi
    mid = lax.reduce_precision(r, 8, 7)
    return hi, mid, r - mid


def _tables(idx, g, E, C):
    t, k = idx.shape
    oh = idx[:, :, None] == jnp.arange(E, dtype=idx.dtype)
    m = jnp.sum(oh, axis=1, dtype=jnp.int32).astype(BF16)
    pos = jnp.arange(t, dtype=jnp.int32)
    tri = (pos[None, :] < pos[:, None]).astype(BF16)
    cnt = jnp.dot(tri, m, preferred_element_type=F32)
    r = jnp.sum(jnp.where(oh, cnt[:, None, :], 0.0), axis=-1)
    ohr = r[:, :, None] == jnp.arange(C, dtype=F32)
    one = jnp.ones((t, k), F32)
    lo = (pos % 256).astype(F32)[:, None] * one
    hi = (pos // 256).astype(F32)[:, None] * one
    vals = jnp.stack((one, hi, lo) + _parts(g), axis=-1)
    rhs = jnp.where(ohr[:, :, None, :], vals[..., None], 0.0).astype(BF16)
    res = jnp.einsum('tje,tjic->iec', oh.astype(BF16), rhs, preferred_element_type=F32)
    tab = jnp.where(res[0] > 0.5, res[1] * 256.0 + res[2], -1.0).astype(jnp.int32)
    return tab, (res[3] + res[4]) + res[5]


def _kernel(O, X, el, C, xall, tab_in, tab_own, g_own, w1, w3, w2, y, stage, recv,
            w1v, w3v, w2v, xs, xt, ob, acc, wsem, xsem, osem, ysem, ssem, rsem):
    n = O * X
    W = X // 2
    T, D = acc.shape
    B = el * C
    G = 2 * W
    NG = n // G
    half = G * C // 2
    mo = lax.axis_index('outer')
    mx = lax.axis_index('expert')
    mc = mx // 2
    core = lax.rem(mx, 2)
    me = mo * X + mx

    def seq(i):
        return lax.rem(2 * i + 1 - 3 * (i // 2) + 4, 4)

    def offs(q, j, c):
        a = seq(j // 2)
        b = seq(lax.rem(j // 2 + q, W))
        return a + c * (b - a), b + c * (a - b)

    def peer(q, j):
        a, b = offs(q, j, core)
        return lax.rem(mo + a, O), 2 * lax.rem(mc + b, W) + lax.rem(core + j % 2, 2)

    def origin(q, j):
        c = lax.rem(core + j % 2, 2)
        a, b = offs(q, j, c)
        return lax.rem(mo - a + O, O), 2 * lax.rem(mc - b + W, W) + c

    def flat(p):
        return p[0] * X + p[1]

    def block(ref, d):
        return ref.at[pl.ds(pl.multiple_of(d * B, B), B)]

    def is_self(q, j):
        return (q == 0) & (j == G - 2)

    bar = pltpu.get_barrier_semaphore()

    def greet(s, _):
        q, j = s // G, lax.rem(s, G)

        @pl.when(jnp.logical_not(is_self(q, j)))
        def _():
            po, px = peer(q, j)
            pl.semaphore_signal(bar, inc=1, device_id={'outer': po, 'expert': px}, device_id_type=MESH)
        return 0

    lax.fori_loop(0, n, greet, 0)

    def wcopies(e):
        return (pltpu.make_async_copy(w1.at[e], w1v.at[e], wsem.at[0, e]),
                pltpu.make_async_copy(w3.at[e], w3v.at[e], wsem.at[1, e]),
                pltpu.make_async_copy(w2.at[e], w2v.at[e], wsem.at[2, e]))

    def xcopy(s, slot):
        src = flat(peer(s // G, lax.rem(s, G)))
        return pltpu.make_async_copy(xall.at[pl.ds(pl.multiple_of(src * T, T), T)], xs.at[slot], xsem.at[slot])

    xcopy(0, 0).start()
    for e in range(el):
        for cp in wcopies(e):
            cp.start()
    pl.semaphore_wait(bar, n - 1)

    def send(q, j):
        po, px = peer(q, j)
        k = q * G + j
        return pltpu.make_async_remote_copy(
            src_ref=block(stage, po * X + px), dst_ref=block(recv, me), send_sem=ssem.at[k],
            recv_sem=rsem.at[k], device_id={'outer': po, 'expert': px}, device_id_type=MESH)

    tok = lax.broadcasted_iota(jnp.int32, (T, B), 0)
    NT = 512

    def group(q, _):
        def pick(j, _):
            s = q * G + j
            slot = lax.rem(s, 2)

            @pl.when(s + 1 < n)
            def _():
                xcopy(s + 1, 1 - slot).start()
            xcopy(s, slot).wait()
            row = tab_in[pl.ds(flat(peer(q, j)), 1), :]
            hot = jnp.where(tok == row, 1.0, 0.0).astype(BF16)
            at = pl.ds(pl.multiple_of(j * C, C), C)
            for c0 in range(0, D, NT):
                r = lax.dot_general(hot, xs[slot, :, c0:c0 + NT], (((0,), (0,)), ((), ())),
                                    preferred_element_type=F32).astype(BF16)
                for e in range(el):
                    xt[e, at, c0:c0 + NT] = r[e * C:(e + 1) * C]
            return 0

        lax.fori_loop(0, G, pick, 0)

        def odrain(slot):
            pltpu.make_async_copy(ob.at[slot], stage.at[pl.ds(0, half)], osem.at[slot]).wait()

        def ffn(i, _):
            e, hh = i // 2, lax.rem(i, 2)

            @pl.when((q == 0) & (hh == 0))
            def _():
                for cp in wcopies(e):
                    cp.wait()
            xr = xt[e, pl.ds(pl.multiple_of(hh * half, half), half), :]
            a = jnp.dot(xr, w1v[e], preferred_element_type=F32)
            b = jnp.dot(xr, w3v[e], preferred_element_type=F32)
            h = (jax.nn.silu(a) * b).astype(BF16)

            @pl.when(i >= 2)
            def _():
                odrain(hh)
            for c0 in range(0, D, NT):
                ob[hh, :, c0:c0 + NT] = jnp.dot(h, w2v[e, :, c0:c0 + NT], preferred_element_type=F32).astype(BF16)
            for jj in range(G // 2):
                d = flat(peer(q, hh * (G // 2) + jj))
                pltpu.make_async_copy(
                    ob.at[hh, pl.ds(jj * C, C)],
                    stage.at[pl.ds(pl.multiple_of(d * B + e * C, C), C)], osem.at[hh]).start()
            return 0

        lax.fori_loop(0, 2 * el, ffn, 0)
        for hh in range(2):
            odrain(hh)

        def go(j, _):
            @pl.when(jnp.logical_not(is_self(q, j)))
            def _():
                send(q, j).start()
            return 0

        lax.fori_loop(0, G, go, 0)
        return 0

    lax.fori_loop(0, NG, group, 0)

    acc[...] = jnp.zeros_like(acc)

    def rcopy(p, i, slot, own):
        q, j = p // W, 2 * lax.rem(p, W) + i
        ref = stage if own else recv
        return pltpu.make_async_copy(block(ref, flat(origin(q, j))), xs.at[slot, pl.ds(i * B, B)], rsem2(slot, i))

    def rsem2(slot, i):
        return ysem.at[2 * slot + i]

    def fetch(p, slot):
        for i in range(2):
            q, j = p // W, 2 * lax.rem(p, W) + i
            k = q * G + j
            if i == 0:
                own = p == W - 1

                @pl.when(own)
                def _():
                    rcopy(p, i, slot, True).start()

                @pl.when(jnp.logical_not(own))
                def _():
                    po, px = origin(q, j)
                    arrive(k, po, px).wait_recv()
                    rcopy(p, i, slot, False).start()
            else:
                po, px = origin(q, j)
                arrive(k, po, px).wait_recv()
                rcopy(p, i, slot, False).start()

    def arrive(k, po, px):
        return pltpu.make_async_remote_copy(
            src_ref=block(stage, po * X + px), dst_ref=block(recv, po * X + px), send_sem=ssem.at[k],
            recv_sem=rsem.at[k], device_id={'outer': po, 'expert': px}, device_id_type=MESH)

    fetch(0, 0)

    def comb(p, _):
        slot = lax.rem(p, 2)

        @pl.when(p + 1 < n // 2)
        def _():
            fetch(p + 1, 1 - slot)
        ws = []
        for i in range(2):
            m = flat(origin(p // W, 2 * lax.rem(p, W) + i))
            w = jnp.where(tok == tab_own[pl.ds(m, 1), :], g_own[pl.ds(m, 1), :], 0.0)
            hi = w.astype(BF16)
            r = w - hi.astype(F32)
            mid = r.astype(BF16)
            lo = (r - mid.astype(F32)).astype(BF16)
            ws.append((hi, mid, lo))
        for i in range(2):
            rcopy(p, i, slot, False).wait()
        lhs = [jnp.concatenate((ws[0][u], ws[1][u]), axis=1) for u in range(3)]
        for c0 in range(0, D, NT):
            rr = xs[slot, :, c0:c0 + NT]
            acc[:, c0:c0 + NT] += (jnp.dot(lhs[0], rr, preferred_element_type=F32)
                                   + jnp.dot(lhs[1], rr, preferred_element_type=F32)
                                   + jnp.dot(lhs[2], rr, preferred_element_type=F32))
        return 0

    lax.fori_loop(0, n // 2, comb, 0)

    ycopies = []
    for hh in range(T // half):
        ob[hh] = acc[hh * half:(hh + 1) * half, :].astype(BF16)
        cp = pltpu.make_async_copy(ob.at[hh], y.at[pl.ds(hh * half, half)], osem.at[hh])
        cp.start()
        ycopies.append(cp)
    for cp in ycopies:
        cp.wait()

    def sent(s, _):
        q, j = s // G, lax.rem(s, G)

        @pl.when(jnp.logical_not(is_self(q, j)))
        def _():
            send(q, j).wait_send()
        return 0

    lax.fori_loop(0, n, sent, 0)


def solution(mesh):
    O = mesh.shape['outer']
    X = mesh.shape['expert']
    n = O * X
    tok = P(('data', 'outer', 'expert'), None)
    wsp = P(('outer', 'expert'), None, None)

    def local(x, wr, idx, w1, w3, w2):
        T, D = x.shape
        k = idx.shape[1]
        E = wr.shape[1]
        el, _, FF = w1.shape
        C = 2 * T * k // E
        B = el * C
        half = X * C // 2
        xall = lax.all_gather(x, ('outer', 'expert'), axis=0, tiled=True)
        g = _gate(x, wr, idx)
        tab, gs = _tables(idx, g, E, C)
        tab_own = tab.reshape(n, B)
        g_own = gs.reshape(n, B)
        tab_in = lax.all_to_all(tab_own, ('outer', 'expert'), 0, 0, tiled=True)
        anyspec = pl.BlockSpec(memory_space=pl.ANY)
        vspec = pl.BlockSpec(memory_space=pltpu.VMEM)
        y, _, _ = pl.pallas_call(
            functools.partial(_kernel, O, X, el, C),
            out_shape=(jax.ShapeDtypeStruct((T, D), BF16),
                       jax.ShapeDtypeStruct((n * B, D), BF16),
                       jax.ShapeDtypeStruct((n * B, D), BF16)),
            in_specs=[anyspec, vspec, vspec, vspec, anyspec, anyspec, anyspec],
            out_specs=(anyspec, anyspec, anyspec),
            scratch_shapes=[
                pltpu.VMEM((el, D, FF), BF16),
                pltpu.VMEM((el, D, FF), BF16),
                pltpu.VMEM((el, FF, D), BF16),
                pltpu.VMEM((2, T, D), BF16),
                pltpu.VMEM((el, X * C, D), BF16),
                pltpu.VMEM((2, half, D), BF16),
                pltpu.VMEM((T, D), F32),
                pltpu.SemaphoreType.DMA((3, el)),
                pltpu.SemaphoreType.DMA((2,)),
                pltpu.SemaphoreType.DMA((2,)),
                pltpu.SemaphoreType.DMA((4,)),
                pltpu.SemaphoreType.DMA((n,)),
                pltpu.SemaphoreType.DMA((n,)),
            ],
            compiler_params=pltpu.CompilerParams(
                collective_id=0, has_side_effects=True, vmem_limit_bytes=67043328),
        )(xall, tab_in, tab_own, g_own, w1, w3, w2)
        return y

    return jax.shard_map(local, mesh=mesh, in_specs=(tok, P(None, None), tok, wsp, wsp, wsp), out_specs=tok, check_vma=False)
```

time: 1900 us -> 669 us (0.35)
  blocking collectives: 1140 us -> 0 us
  Pallas kernels: 0 us -> 447 us
  local copies, waits for them, and re-layouts: 245 us -> 6.07 us
  matrix products: 196 us -> 2.14 us
  waiting for transfers between devices: 249 us -> 185 us
  other arithmetic: 43.6 us -> 3.58 us
    all_to_all x3 -> x0, blocking collectives: 1140 us -> none  [the longest x1 382 us: local(): buf = lax.all_to_all(buf, 'outer', 0, 0, tiled=True)]
    pallas_call x0 -> x1, Pallas kernels: none -> 447 us  [local(): pl.pallas_call(functools.partial(_kernel, O, X, el, C), out_shape=(jax.Sh...]
    all_to_all x1, waiting for transfers between devices: 249 us -> 5.52 us  [local(): tab_in = lax.all_to_all(tab_own, ('outer', 'expert'), 0, 0, tiled=True)]
    dot_general x7 -> x3, matrix products: 196 us -> 2.14 us  [the longest x1 1.13 us: _tables(): jnp.einsum('tje,tjic->iec', oh.astype(BF16), rhs, preferred_element_type=...]
    all_gather x0 -> x1, waiting for transfers between devices: none -> 179 us  [local(): xall = lax.all_gather(x, ('outer', 'expert'), axis=0, tiled=True)]
    all_to_all x3 -> x0, local copies, waits for them, and re-layouts: 68.8 us -> none  [the longest x1 22.9 us: local(): buf = lax.all_to_all(buf, 'expert', 1, 1, tiled=True)]
    reshape x2 -> x0, local copies, waits for them, and re-layouts: 45.9 us -> none  [the longest x1 23 us: local(): o = o.reshape(el, n, C, dm).transpose(1, 0, 2, 3).reshape(O, X, el * C, dm)]
    convert_element_type x1 -> x3, local copies, waits for them, and re-layouts: 30 us -> 1.49 us  [_tables(): jnp.where(res[0] > 0.5, res[1] * 256.0 + res[2], -1.0).astype(jnp.int32)]
  transfers between devices with their start and end apart: 1 -> 2, of which waited for: 1 -> 2; matrix products, arithmetic and copies ran while one was open for 6% -> 1% of each run, Pallas kernels for 0% -> 0%
where the time goes in v1:
time: 669 us; the launch traced here: 666 us
  Pallas kernels  447 us (67%)
  waiting for transfers between devices  185 us (28%)
  between operations  13.6 us (2%)
  starting transfers between devices  9.14 us (1%)
    pallas_call x1, Pallas kernels, local(): pl.pallas_call(functools.partial(_kernel, O, X, el, C), out_shape=(jax.Sh...  447 us
    all_gather x1, waiting for transfers between devices, local(): xall = lax.all_gather(x, ('outer', 'expert'), axis=0, tiled=True)  179 us
  transfers between devices with their start and end apart: 2, of which 2 were waited for; matrix products, arithmetic and copies ran while one was open for 1% of the time, Pallas kernels for 0%

profile of v1, /device:TPU:97, one launch (start us, length us, event | category | flops | bytes accessed | tf_op | source)
XLA Modules:
  0.0 666.2 jit_solution(599204319173313097)
XLA Ops:
  6.5 0.0 copy-start
  6.6 0.0 all-gather.2.cloned.1.call-start
  6.6 0.7 all-gather.2.cloned.1.call-update
  7.3 0.0 copy-start.2
  7.3 1.5 convert_reduce_fusion
  8.8 0.3 fusion.10
  9.1 0.0 copy-done
  9.1 0.0 copy-done.1
  9.1 0.7 fusion.27
  9.8 0.0 copy-done.2
  9.8 1.9 select_reduce_fusion.1
  11.9 0.1 iota_compare_fusion.1
  12.0 1.1 fusion.6
  13.2 0.1 copy.13
  13.3 0.7 convert_element_type.50
  14.0 9.1 %all-to-all-start = ((s32[32,1,256]{2,1,0:T(1,128)}), s32[32,1,256]{2,1,0:T(1,128)S(1)}, u32[]{:S(2)}, u32[]{:S(2)}) async-start(s32[32,1,256]{2,1,0:T(1,128)} %convert_element_type.50), calls=%async_computation | async-start | bytes 65536 | tf_op jit(solution)/shard_map/all_to_all | solution.py:294
  23.2 0.7 convert_element_type.49.tab_own
  23.8 0.1 copy.16
  23.9 0.7 add.44.g_own
  24.6 5.5 all-to-all-done
  30.1 0.6 copy.20
  30.8 178.9 %all-gather.2.cloned.1.call-done.xall = bf16[16384,2048]{1,0:T(8,128)(2,1)} async-done(((bf16[512,2048]{1,0:T(8,128)(2,1)}), bf16[16384,2048]{1,0:T(8,128)(2,1)}) %all-gather.2.cloned.1.call-update) | async-done | bytes 67108880 | tf_op jit(solution)/shard_map/all_gather | solution.py:289
  209.7 446.5 %shard_map.64 = (bf16[512,2048]{1,0:T(8,128)(2,1)}, bf16[8192,2048]{1,0:T(8,128)(2,1)}, bf16[8192,2048]{1,0:T(8,128)(2,1)}) custom-call(bf16[16384,2048]{1,0:T(8,128)(2,1)} %all-gather.2.cloned.1.call-done.xall, s32[32,256]{1,0:T(8,128)} %bitcast.27, s32[32,256]{1,0:T(8,128)} %convert_element_type.49.tab_own, f32[32,256]{1,0:T(8,128)} %add.44.g_own, ...), custom_call_target="tpu_custom_call" | custom-call | tf_op jit(solution)/shard_map/pallas_call | solution.py:297
  656.2 3.2 copy.27
  (12 shorter events, 0.1 us)
Async XLA Ops:
  6.5 2.5 copy-start
  6.5 2.6 copy-start.1
  6.6 203.1 %all-gather.2.cloned.1.call-start = ((), (), s32[]{:S(2)}) async-start(), calls=%async_computation.1 | async-start | bytes 69206016 | tf_op jit(solution)/shard_map/all_gather | solution.py:289
  7.3 2.5 copy-start.2
  14.0 16.1 %all-to-all-start = ((s32[32,1,256]{2,1,0:T(1,128)}), s32[32,1,256]{2,1,0:T(1,128)S(1)}, u32[]{:S(2)}, u32[]{:S(2)}) async-start(s32[32,1,256]{2,1,0:T(1,128)} %convert_element_type.50), calls=%async_computation | async-start | bytes 65536 | tf_op jit(solution)/shard_map/all_to_all | solution.py:294
Sparse Core Ops, SparseCore 0:
  9.4 200.1 all-gather.1

commit v2 on v0

v2 whole, which is shorter than its diff:
```python
import functools

import jax
import jax.numpy as jnp
from jax import lax
from jax.experimental import pallas as pl
from jax.experimental.pallas import tpu as pltpu
from jax.sharding import PartitionSpec as P

MESH = pl.DeviceIdType.MESH
F32 = jnp.float32
BF16 = jnp.bfloat16


def _gate(x, wr, idx):
    logits = jnp.dot(x, wr, preferred_element_type=F32)
    oh = idx[:, :, None] == jnp.arange(wr.shape[1], dtype=idx.dtype)
    return jax.nn.softmax(jnp.sum(jnp.where(oh, logits[:, None, :], 0.0), axis=-1), axis=-1)


def _parts(w):
    hi = lax.reduce_precision(w, 8, 7)
    r = w - hi
    mid = lax.reduce_precision(r, 8, 7)
    return hi, mid, r - mid


def _tables(idx, g, E, C):
    t, k = idx.shape
    oh = idx[:, :, None] == jnp.arange(E, dtype=idx.dtype)
    m = jnp.sum(oh, axis=1, dtype=jnp.int32).astype(BF16)
    pos = jnp.arange(t, dtype=jnp.int32)
    tri = (pos[None, :] < pos[:, None]).astype(BF16)
    cnt = jnp.dot(tri, m, preferred_element_type=F32)
    r = jnp.sum(jnp.where(oh, cnt[:, None, :], 0.0), axis=-1)
    ohr = r[:, :, None] == jnp.arange(C, dtype=F32)
    one = jnp.ones((t, k), F32)
    lo = (pos % 256).astype(F32)[:, None] * one
    hi = (pos // 256).astype(F32)[:, None] * one
    vals = jnp.stack((one, hi, lo) + _parts(g), axis=-1)
    rhs = jnp.where(ohr[:, :, None, :], vals[..., None], 0.0).astype(BF16)
    res = jnp.einsum('tje,tjic->iec', oh.astype(BF16), rhs, preferred_element_type=F32)
    tab = jnp.where(res[0] > 0.5, res[1] * 256.0 + res[2], -1.0).astype(jnp.int32)
    return tab, (res[3] + res[4]) + res[5]


def _kernel(O, X, el, C, xall, tab_in, pk_a, pk_b, w1, w3, w2, y, stage, recv, part,
            xs, ob, wsem, xsem, osem, ssem, rsem, pssem, prsem):
    n = O * X
    W = X // 2
    _, T, D = xs.shape
    H = D // 2
    FF = w1.shape[2]
    B = el * C
    G = 2 * W
    NG = n // G
    half = G * C // 2
    NT = 512
    mo = lax.axis_index('outer')
    mx = lax.axis_index('expert')
    mc = mx // 2
    core = lax.rem(mx, 2)

    def offs(q, i):
        u, v = lax.rem(i, 2), lax.rem(i // 2, 2)
        return 1 - q // 2 + 2 * u, 1 - lax.rem(q, 2) + 2 * lax.rem(u + v, 2)

    def dest(q, j):
        a, b = offs(q, j // 2)
        return lax.rem(mo + a, O), lax.rem(mc + b, W), lax.rem(core + j % 2, 2)

    def block(ref, d):
        return ref.at[pl.ds(pl.multiple_of(d * B, B), B)]

    def at_a(yd, sx):
        return yd * X + sx

    def at_b(xd, sy, sc):
        return xd * X + sy * 2 + sc

    bar = pltpu.get_barrier_semaphore()

    def greet(po, px):
        pl.semaphore_signal(bar, inc=1, device_id={'outer': po, 'expert': px}, device_id_type=MESH)

    for d in range(1, X):
        greet(mo, lax.rem(mx + d, X))
    for a in range(1, O):
        for c in range(2):
            greet(lax.rem(mo + a, O), 2 * mc + c)

    def xcopy(s, slot):
        yd, xd, cd = dest(s // G, lax.rem(s, G))
        src = yd * X + 2 * xd + cd
        return pltpu.make_async_copy(xall.at[pl.ds(pl.multiple_of(src * T, T), T)], xs.at[slot], xsem.at[slot])

    def send_a(q, j):
        yd, xd, cd = dest(q, j)
        return pltpu.make_async_remote_copy(
            src_ref=block(stage.at[0], yd * X + 2 * xd + cd), dst_ref=block(recv.at[0], at_a(yd, mx)),
            send_sem=ssem.at[0, q * G + j], recv_sem=rsem.at[0, q * G + j],
            device_id={'outer': mo, 'expert': 2 * xd + cd}, device_id_type=MESH)

    def send_b(q, j):
        yd, xd, cd = dest(q, j)
        return pltpu.make_async_remote_copy(
            src_ref=block(stage.at[1], yd * X + 2 * xd + cd), dst_ref=block(recv.at[1], at_b(xd, mo, core)),
            send_sem=ssem.at[1, q * G + j], recv_sem=rsem.at[1, q * G + j],
            device_id={'outer': yd, 'expert': 2 * mc + cd}, device_id_type=MESH)

    def away(q, j):
        a, b = offs(q, j // 2)
        k = j % 2
        return b + k > 0, a + k > 0

    def experts(w1v, w3v, w2v, xt):
        def wcopies(e):
            return (pltpu.make_async_copy(w1.at[e], w1v.at[e], wsem.at[0, e]),
                    pltpu.make_async_copy(w3.at[e], w3v.at[e], wsem.at[1, e]),
                    pltpu.make_async_copy(w2.at[e], w2v.at[e], wsem.at[2, e]))

        xcopy(0, 0).start()
        for e in range(el):
            for cp in wcopies(e):
                cp.start()
        pl.semaphore_wait(bar, X - 1 + 2 * (O - 1))
        tok = lax.broadcasted_iota(jnp.int32, (T, B), 0)

        def group(q, _):
            def pick(j, _):
                s = q * G + j
                slot = lax.rem(s, 2)

                @pl.when(s + 1 < n)
                def _():
                    xcopy(s + 1, 1 - slot).start()
                xcopy(s, slot).wait()
                yd, xd, cd = dest(q, j)
                row = tab_in[pl.ds(yd * X + 2 * xd + cd, 1), :]
                hot = jnp.where(tok == row, 1.0, 0.0).astype(BF16)
                at = pl.ds(pl.multiple_of(j * C, C), C)
                for c0 in range(0, D, NT):
                    r = lax.dot_general(hot, xs[slot, :, c0:c0 + NT], (((0,), (0,)), ((), ())),
                                        preferred_element_type=F32).astype(BF16)
                    for e in range(el):
                        xt[e, at, c0:c0 + NT] = r[e * C:(e + 1) * C]
                return 0

            lax.fori_loop(0, G, pick, 0)

            def odrain(hh):
                for v in range(2):
                    pltpu.make_async_copy(ob.at[hh, :, pl.ds(v * H, H)], stage.at[v, pl.ds(0, half)],
                                          osem.at[hh, v]).wait()

            def ffn(i, _):
                e, hh = i // 2, lax.rem(i, 2)

                @pl.when((q == 0) & (hh == 0))
                def _():
                    for cp in wcopies(e):
                        cp.wait()
                xr = xt[e, pl.ds(pl.multiple_of(hh * half, half), half), :]
                a = jnp.dot(xr, w1v[e], preferred_element_type=F32)
                b = jnp.dot(xr, w3v[e], preferred_element_type=F32)
                h = (jax.nn.silu(a) * b).astype(BF16)

                @pl.when(i >= 2)
                def _():
                    odrain(hh)
                for c0 in range(0, D, NT):
                    ob[hh, :, c0:c0 + NT] = jnp.dot(h, w2v[e, :, c0:c0 + NT],
                                                    preferred_element_type=F32).astype(BF16)
                for jj in range(G // 2):
                    yd, xd, cd = dest(q, hh * (G // 2) + jj)
                    at = pl.ds(pl.multiple_of((yd * X + 2 * xd + cd) * B + e * C, C), C)
                    for v in range(2):
                        pltpu.make_async_copy(ob.at[hh, pl.ds(jj * C, C), pl.ds(v * H, H)],
                                              stage.at[v, at], osem.at[hh, v]).start()
                return 0

            lax.fori_loop(0, 2 * el, ffn, 0)
            for hh in range(2):
                odrain(hh)

            def go(j, _):
                far_a, far_b = away(q, j)

                @pl.when(far_a)
                def _():
                    send_a(q, j).start()

                @pl.when(far_b)
                def _():
                    send_b(q, j).start()
                return 0

            lax.fori_loop(0, G, go, 0)
            return 0

        lax.fori_loop(0, NG, group, 0)

    pl.run_scoped(experts, pltpu.VMEM((el, D, FF), BF16), pltpu.VMEM((el, D, FF), BF16),
                  pltpu.VMEM((el, FF, D), BF16), pltpu.VMEM((el, G * C, D), BF16))

    def combine(pa, pb):
        pa[...] = jnp.zeros_like(pa)
        pb[...] = jnp.zeros_like(pb)
        tokf = lax.broadcasted_iota(jnp.int32, (T, 2 * B), 0).astype(F32)

        def origins(p):
            a, b = offs(p // W, lax.rem(p, W))
            return a, b, lax.rem(mo - a + O, O), lax.rem(mc - b + W, W)

        def fetch(p, slot):
            a, b, sy, sx = origins(p)
            yd, xd = lax.rem(mo + a, O), lax.rem(mc + b, W)
            for k in range(2):
                q, j = p // W, 2 * lax.rem(p, W) + k
                c = lax.rem(core + k, 2)
                at = pl.ds(pl.multiple_of(c * B, B), B)
                for v in range(2):
                    if v == 0:
                        src, own = block(recv.at[0], at_a(yd, 2 * sx + c)), block(stage.at[0], yd * X + 2 * mc + core)
                    else:
                        src, own = block(recv.at[1], at_b(xd, sy, c)), block(stage.at[1], mo * X + 2 * xd + core)
                    far = (b if v == 0 else a) > 0

                    def bring(ref, v=v, at=at):
                        pltpu.make_async_copy(ref, xs.at[slot, at, pl.ds(v * H, H)], xsem.at[slot]).start()

                    def take(src=src, v=v, j=j, bring=bring):
                        pltpu.make_async_remote_copy(
                            src_ref=src, dst_ref=src, send_sem=ssem.at[v, q * G + j],
                            recv_sem=rsem.at[v, q * G + j],
                            device_id={'outer': mo, 'expert': lax.rem(mx + 1, X)},
                            device_id_type=MESH).wait_recv()
                        bring(src)
                    if k == 1:
                        take()
                    else:
                        pl.when(far)(take)
                        pl.when(jnp.logical_not(far))(functools.partial(bring, own))

        def psend(v, d):
            if v == 0:
                src, to = pa.at[d], {'outer': lax.rem(mo + d, O), 'expert': mx}
            else:
                src, to = pb.at[d], {'outer': mo, 'expert': 2 * lax.rem(mc + d, W) + core}
            return pltpu.make_async_remote_copy(
                src_ref=src, dst_ref=part.at[v, d - 1], send_sem=pssem.at[v, d - 1],
                recv_sem=prsem.at[v, d - 1], device_id=to, device_id_type=MESH)

        fetch(0, 0)

        def weights(ref, d, r0):
            out = []
            rows = [ref[d, 0, pl.ds(r0 + c, 1), :] for c in range(2)]
            gs = [ref[d, 1, pl.ds(r0 + c, 1), :] for c in range(2)]
            w = jnp.where(tokf == jnp.concatenate(rows, axis=1), jnp.concatenate(gs, axis=1), 0.0)
            hi = w.astype(BF16)
            r = w - hi.astype(F32)
            mid = r.astype(BF16)
            return hi, mid, (r - mid.astype(F32)).astype(BF16)

        def comb(p, _):
            slot = lax.rem(p, 2)

            @pl.when(p + 1 < n // 2)
            def _():
                fetch(p + 1, 1 - slot)
            a, b, sy, sx = origins(p)
            wa = weights(pk_a, lax.rem(mo + a, O), 2 * sx)
            wb = weights(pk_b, 2 * lax.rem(mc + b, W) + core, 2 * sy)
            pltpu.make_async_copy(xall.at[pl.ds(0, T)], xs.at[slot], xsem.at[slot]).wait()
            for acc, d, ws, base in ((pa, a, wa, 0), (pb, b, wb, H)):
                for c0 in range(0, H, NT):
                    rr = xs[slot, :, base + c0:base + c0 + NT]
                    acc[d, :, c0:c0 + NT] += (jnp.dot(ws[0], rr, preferred_element_type=F32)
                                              + jnp.dot(ws[1], rr, preferred_element_type=F32)
                                              + jnp.dot(ws[2], rr, preferred_element_type=F32))
            for last, v, ds in ((2 * W - 1, 0, (1, 3)), (3 * W - 1, 1, (1, 3)), (4 * W - 1, 0, (2,)), (4 * W - 1, 1, (2,))):
                @pl.when(p == last)
                def _(v=v, ds=ds):
                    for d in ds:
                        psend(v, d).start()
            return 0

        lax.fori_loop(0, n // 2, comb, 0)

        def sent(s, _):
            q, j = s // G, lax.rem(s, G)
            far_a, far_b = away(q, j)

            @pl.when(far_a)
            def _():
                send_a(q, j).wait_send()

            @pl.when(far_b)
            def _():
                send_b(q, j).wait_send()
            return 0

        lax.fori_loop(0, n, sent, 0)

        accs = (pa, pb)
        for d in (1, 3, 2):
            for v in range(2):
                psend(v, d).wait()
                pltpu.make_async_copy(part.at[v, d - 1], accs[v].at[d], prsem.at[v, d - 1]).start()
            for v in range(2):
                pltpu.make_async_copy(part.at[v, d - 1], accs[v].at[d], prsem.at[v, d - 1]).wait()
                if d != 2:
                    accs[v][0] += accs[v][d]
        for v in range(2):
            for hh in range(T // half):
                rows = slice(hh * half, (hh + 1) * half)
                ob[hh, :, v * H:(v + 1) * H] = (accs[v][0, rows] + accs[v][2, rows]).astype(BF16)
        cps = [pltpu.make_async_copy(ob.at[hh], y.at[pl.ds(hh * half, half)], osem.at[hh, 0])
               for hh in range(T // half)]
        for cp in cps:
            cp.start()
        for cp in cps:
            cp.wait()

    pl.run_scoped(combine, pltpu.VMEM((O, T, H), F32), pltpu.VMEM((W, T, H), F32))


def solution(mesh):
    O = mesh.shape['outer']
    X = mesh.shape['expert']
    n = O * X
    tok = P(('data', 'outer', 'expert'), None)
    wsp = P(('outer', 'expert'), None, None)

    def local(x, wr, idx, w1, w3, w2):
        T, D = x.shape
        k = idx.shape[1]
        E = wr.shape[1]
        el, _, FF = w1.shape
        C = 2 * T * k // E
        B = el * C
        half = X * C // 2
        xall = lax.all_gather(x, ('outer', 'expert'), axis=0, tiled=True)
        g = _gate(x, wr, idx)
        tab, gs = _tables(idx, g, E, C)
        tab_in = lax.all_to_all(tab.reshape(n, B), ('outer', 'expert'), 0, 0, tiled=True)
        pk = jnp.stack((tab.astype(F32).reshape(n, B), gs.reshape(n, B)))
        pk_a = lax.all_to_all(pk.reshape(2, O, X, B).transpose(1, 0, 2, 3), 'outer', 0, 0, tiled=True)
        pk_b = pk.reshape(2, O, X // 2, 2, B).transpose(2, 0, 1, 3, 4).reshape(X // 2, 1, 2, 2 * O, B)
        pk_b = jnp.broadcast_to(pk_b, (X // 2, 2, 2, 2 * O, B)).reshape(X, 2, 2 * O, B)
        pk_b = lax.all_to_all(pk_b, 'expert', 0, 0, tiled=True)
        anyspec = pl.BlockSpec(memory_space=pl.ANY)
        vspec = pl.BlockSpec(memory_space=pltpu.VMEM)
        y = pl.pallas_call(
            functools.partial(_kernel, O, X, el, C),
            out_shape=(jax.ShapeDtypeStruct((T, D), BF16),
                       jax.ShapeDtypeStruct((2, n * B, D // 2), BF16),
                       jax.ShapeDtypeStruct((2, n * B, D // 2), BF16),
                       jax.ShapeDtypeStruct((2, O - 1, T, D // 2), F32)),
            in_specs=[anyspec, vspec, vspec, vspec, anyspec, anyspec, anyspec],
            out_specs=(anyspec,) * 4,
            scratch_shapes=[
                pltpu.VMEM((2, T, D), BF16),
                pltpu.VMEM((2, half, D), BF16),
                pltpu.SemaphoreType.DMA((3, el)),
                pltpu.SemaphoreType.DMA((2,)),
                pltpu.SemaphoreType.DMA((2, 2)),
                pltpu.SemaphoreType.DMA((2, n)),
                pltpu.SemaphoreType.DMA((2, n)),
                pltpu.SemaphoreType.DMA((2, O - 1)),
                pltpu.SemaphoreType.DMA((2, O - 1)),
            ],
            compiler_params=pltpu.CompilerParams(
                collective_id=0, has_side_effects=True, vmem_limit_bytes=67043328),
        )(xall, tab_in, pk_a, pk_b, w1, w3, w2)
        return y[0]

    return jax.shard_map(local, mesh=mesh, in_specs=(tok, P(None, None), tok, wsp, wsp, wsp), out_specs=tok, check_vma=False)
```

time: 1900 us -> 570 us (0.30)
  the two profiles are of different devices: /device:TPU:97 before, /device:TPU:121 now
where the time goes in v2:
time: 570 us; the launch traced here: 569 us
  Pallas kernels  353 us (62%)
  waiting for transfers between devices  173 us (30%)
  starting transfers between devices  17.3 us (3%)
  between operations  13.6 us (2%)
  local copies, waits for them, and re-layouts  5.86 us (1%)
    pallas_call x1, Pallas kernels, local(): pl.pallas_call(functools.partial(_kernel, O, X, el, C), out_shape=(jax.Sh...  353 us
    all_gather x1, waiting for transfers between devices, local(): xall = lax.all_gather(x, ('outer', 'expert'), axis=0, tiled=True)  159 us
  transfers between devices with their start and end apart: 4, of which 4 were waited for; matrix products, arithmetic and copies ran while one was open for 2% of the time, Pallas kernels for 0%

profile of v2, /device:TPU:121, one launch (start us, length us, event | category | flops | bytes accessed | tf_op | source)
XLA Modules:
  0.0 568.9 jit_solution(13539034851580946905)
XLA Ops:
  6.6 0.7 all-gather.2.cloned.1.call-update
  7.3 1.5 convert_reduce_fusion
  8.8 0.3 fusion.10
  9.1 0.7 fusion.29
  9.8 1.9 select_reduce_fusion.1
  11.9 0.1 iota_compare_fusion.1
  12.0 1.1 fusion.6
  13.2 0.1 copy.26
  13.3 0.7 convert_element_type.93
  14.0 6.7 %all-to-all-start = ((s32[32,1,256]{2,1,0:T(1,128)}), s32[32,1,256]{2,1,0:T(1,128)S(1)}, u32[]{:S(2)}, u32[]{:S(2)}) async-start(s32[32,1,256]{2,1,0:T(1,128)} %convert_element_type.93), calls=%async_computation | async-start | bytes 65536 | tf_op jit(solution)/shard_map/all_to_all | solution.py:347
  20.7 0.1 copy.28
  20.9 0.1 copy.29
  21.1 0.6 maximum_bitcast_fusion
  21.8 0.1 add.93
  21.9 3.9 all-to-all-done
  25.8 5.1 all-to-all-start.1
  31.0 3.1 all-to-all-done.1.pk_a
  34.1 0.7 broadcast_in_dim.73
  34.8 5.4 all-to-all-start.2
  40.2 0.6 copy.39
  40.9 5.9 %all-to-all-done.2.pk_b = f32[8,2,8,256]{3,2,1,0:T(8,128)} async-done(((f32[8,2,8,256]{3,2,1,0:T(8,128)}), f32[8,2,8,256]{3,2,1,0:T(8,128)}, u32[]{:S(2)}, u32[]{:S(2)}) %all-to-all-start.2) | async-done | bytes 131104 | tf_op jit(solution)/shard_map/all_to_all | solution.py:352
  46.8 159.3 %all-gather.2.cloned.1.call-done.xall = bf16[16384,2048]{1,0:T(8,128)(2,1)} async-done(((bf16[512,2048]{1,0:T(8,128)(2,1)}), bf16[16384,2048]{1,0:T(8,128)(2,1)}) %all-gather.2.cloned.1.call-update) | async-done | bytes 67108880 | tf_op jit(solution)/shard_map/all_gather | solution.py:344
  206.1 352.8 %shard_map.64 = (bf16[512,2048]{1,0:T(8,128)(2,1)}, bf16[2,8192,1024]{2,1,0:T(8,128)(2,1)}, bf16[2,8192,1024]{2,1,0:T(8,128)(2,1)}, f32[2,3,512,1024]{3,2,1,0:T(8,128)}) custom-call(bf16[16384,2048]{1,0:T(8,128)(2,1)} %all-gather.2.cloned.1.call-done.xall, s32[32,256]{1,0:T(8,128)} %bitcast.36, f32[4,2,8,256]{3,2,1,0:T(8,128)} %copy-done.2, ...), custom_call_target="tpu_custom_call" | custom-call | tf_op jit(solution)/shard_map/pallas_call | solution.py:355
  558.9 3.2 copy.46
  (26 shorter events, 0.5 us)
Async XLA Ops:
  6.5 2.5 copy-start
  6.5 2.6 copy-start.1
  6.6 199.6 %all-gather.2.cloned.1.call-start = ((), (), s32[]{:S(2)}) async-start(), calls=%async_computation.3 | async-start | bytes 69206016 | tf_op jit(solution)/shard_map/all_gather | solution.py:344
  7.3 2.5 copy-start.3
  14.0 11.8 %all-to-all-start = ((s32[32,1,256]{2,1,0:T(1,128)}), s32[32,1,256]{2,1,0:T(1,128)S(1)}, u32[]{:S(2)}, u32[]{:S(2)}) async-start(s32[32,1,256]{2,1,0:T(1,128)} %convert_element_type.93), calls=%async_computation | async-start | bytes 65536 | tf_op jit(solution)/shard_map/all_to_all | solution.py:347
  25.8 8.4 %all-to-all-start.1 = ((f32[4,2,8,256]{3,2,1,0:T(8,128)}), f32[4,2,8,256]{3,2,1,0:T(8,128)S(1)}, u32[]{:S(2)}, u32[]{:S(2)}) async-start(f32[4,2,8,256]{3,2,1,0:T(8,128)} %maximum_bitcast_fusion), calls=%async_computation.1 | async-start | bytes 131072 | tf_op jit(solution)/shard_map/all_to_all | solution.py:349
  34.1 0.7 copy-start.2
  34.8 12.0 %all-to-all-start.2 = ((f32[8,2,8,256]{3,2,1,0:T(8,128)}), f32[8,2,8,256]{3,2,1,0:T(8,128)}, u32[]{:S(2)}, u32[]{:S(2)}) async-start(f32[8,2,8,256]{3,2,1,0:T(8,128)} %bitcast.11), calls=%async_computation.2 | async-start | bytes 262144 | tf_op jit(solution)/shard_map/all_to_all | solution.py:352
Sparse Core Ops, SparseCore 0:
  9.4 196.6 all-gather.1

commit v3 on v2

v3 whole, which is shorter than its diff:
```python
import functools

import jax
import jax.numpy as jnp
from jax import lax
from jax.experimental import pallas as pl
from jax.experimental.pallas import tpu as pltpu
from jax.sharding import PartitionSpec as P

MESH = pl.DeviceIdType.MESH
F32 = jnp.float32
BF16 = jnp.bfloat16


def _gate(x, wr, idx):
    logits = jnp.dot(x, wr, preferred_element_type=F32)
    oh = idx[:, :, None] == jnp.arange(wr.shape[1], dtype=idx.dtype)
    return jax.nn.softmax(jnp.sum(jnp.where(oh, logits[:, None, :], 0.0), axis=-1), axis=-1)


def _parts(w):
    hi = lax.reduce_precision(w, 8, 7)
    r = w - hi
    mid = lax.reduce_precision(r, 8, 7)
    return hi, mid, r - mid


def _tables(idx, g, E, C):
    t, k = idx.shape
    oh = idx[:, :, None] == jnp.arange(E, dtype=idx.dtype)
    m = jnp.sum(oh, axis=1, dtype=jnp.int32).astype(BF16)
    pos = jnp.arange(t, dtype=jnp.int32)
    tri = (pos[None, :] < pos[:, None]).astype(BF16)
    cnt = jnp.dot(tri, m, preferred_element_type=F32)
    r = jnp.sum(jnp.where(oh, cnt[:, None, :], 0.0), axis=-1)
    ohr = r[:, :, None] == jnp.arange(C, dtype=F32)
    one = jnp.ones((t, k), F32)
    lo = (pos % 256).astype(F32)[:, None] * one
    hi = (pos // 256).astype(F32)[:, None] * one
    vals = jnp.stack((one, hi, lo) + _parts(g), axis=-1)
    rhs = jnp.where(ohr[:, :, None, :], vals[..., None], 0.0).astype(BF16)
    res = jnp.einsum('tje,tjic->iec', oh.astype(BF16), rhs, preferred_element_type=F32)
    tab = jnp.where(res[0] > 0.5, res[1] * 256.0 + res[2], -1.0).astype(jnp.int32)
    return tab, (res[3] + res[4]) + res[5]


ORDER = ((0, 1), (0, 3), (1, 0), (3, 0), (0, 0), (0, 2), (1, 1), (3, 3),
         (1, 3), (3, 1), (1, 2), (3, 2), (2, 1), (2, 3), (2, 0), (2, 2))


def _lut(vals, i):
    r = vals[0]
    for k in range(1, len(vals)):
        r = jnp.where(i == k, vals[k], r)
    return r


def _relays(h, off):
    u, v = off
    if v == 0:
        if u == 3:
            return ((0, 1, 0), (1, 1, None), (1, 3, None))
        if u == 1:
            return ((0, 3, 1), (1, 1, None), (1, 3, None))
        return ((1, 1, None), (1, 3, None))
    if v == 3:
        return ((1, 1, 0),)
    if v == 1:
        return ((1, 3, 1),)
    return ()


def _numbered():
    full, piece = {}, {}
    for h in range(2):
        for d in (1, 3):
            for axis in range(2):
                full[(h, (0, 0), axis, d)] = len(full)
        for u in range(4):
            for v in range(4):
                if (u, v) != (0, 0):
                    for axis, d, part in _relays(h, (u, v)):
                        table = full if part is None else piece
                        table[(h, (u, v), axis, d)] = len(table)
    return full, piece


FULL, PIECE = _numbered()


def _kernel(O, X, el, C, x, pk, w1, w3, w2, y, xall, stage, recv, part,
            xs, ob, tab_in, pk_a, pk_b, wsem, xsem, osem, ssem, rsem, pssem, prsem,
            bsem, bpsem, gsem, gpsem, dsem, hsem, tsem, tsem2):
    n = O * X
    W = X // 2
    _, T, D = xs.shape
    H = D // 2
    FF = w1.shape[2]
    B = el * C
    G = 4
    NG = n // G
    half = G * C
    NT = 512
    mo = lax.axis_index('outer')
    mx = lax.axis_index('expert')
    mc = mx // 2
    core = lax.rem(mx, 2)
    me = mo * X + mx

    def offs(p):
        return _lut([o[0] for o in ORDER], p), _lut([o[1] for o in ORDER], p)

    def dest(s):
        a, b = offs(s // 2)
        return lax.rem(mo + a, O), lax.rem(mc + b, W), lax.rem(core + lax.rem(s, 2), 2)

    def block(ref, d):
        return ref.at[pl.ds(pl.multiple_of(d * B, B), B)]

    def at_a(yd, sx):
        return yd * X + sx

    def at_b(xd, sy, sc):
        return xd * X + sy * 2 + sc

    bar = pltpu.get_barrier_semaphore()

    def greet(d, _):
        t = lax.rem(me + d, n)
        pl.semaphore_signal(bar, inc=1, device_id={'outer': t // X, 'expert': lax.rem(t, X)}, device_id_type=MESH)
        return 0

    lax.fori_loop(1, n, greet, 0)

    def rows(ref, a, b, h, piece, c=None):
        src = lax.rem(mo + a, O) * X + 2 * lax.rem(mc + b, W) + (core if c is None else c)
        step = T // 2
        if piece is None:
            return ref.at[pl.ds(pl.multiple_of(src * T + h * step, step), step)]
        return ref.at[pl.ds(pl.multiple_of(src * T + h * step + piece * (step // 2), step // 2), step // 2)]

    def neighbour(h, axis, d):
        if (axis == 0) == (h == 0):
            return {'outer': mo, 'expert': 2 * lax.rem(mc + d, W) + core}
        return {'outer': lax.rem(mo + d, O), 'expert': mx}

    def offset(h, off):
        return (off[1], off[0]) if h == 0 else off

    def relay(h, off, axis, d, piece, src=None):
        a, b = offset(h, off)
        key = (h, off, axis, d)
        send = gsem.at[FULL[key]] if piece is None else gpsem.at[PIECE[key]]
        u, v = off
        seen = ((u - d) % 4, v) if axis == 0 else (u, (v - d) % 4)
        ra, rb = offset(h, seen)
        k = h * 16 + ra * 4 + rb
        recv_ = bsem.at[k] if piece is None else bpsem.at[2 * k + piece]
        dst = rows(xall, a, b, h, piece)
        pltpu.make_async_remote_copy(src_ref=dst if src is None else src, dst_ref=dst, send_sem=send, recv_sem=recv_,
                                     device_id=neighbour(h, axis, d), device_id_type=MESH).start()

    def share(h, off, src=None):
        a, b = offset(h, off)
        dst = rows(xall, a, b, h, None)
        pltpu.make_async_remote_copy(
            src_ref=dst if src is None else src, dst_ref=dst, send_sem=hsem.at[h * 16 + a * 4 + b],
            recv_sem=dsem.at[a * 4 + b], device_id={'outer': mo, 'expert': 2 * mc + 1 - core},
            device_id_type=MESH).start()

    def other():
        return {'outer': mo, 'expert': 2 * mc + 1 - core}

    def arrive(ref, sem):
        pltpu.make_async_remote_copy(src_ref=ref, dst_ref=ref, send_sem=hsem.at[0], recv_sem=sem,
                                     device_id=other(), device_id_type=MESH).wait_recv()

    def event(h, off):
        a, b = offset(h, off)
        k = h * 16 + a * 4 + b
        if off[1] == 2 or off == (2, 0):
            for piece in range(2):
                arrive(rows(xall, a, b, h, piece), bpsem.at[2 * k + piece])
        else:
            arrive(rows(xall, a, b, h, None), bsem.at[k])
        for axis, d, piece in _relays(h, off):
            relay(h, off, axis, d, piece)
        share(h, off)

    def xcopy(s, slot):
        yd, xd, cd = dest(s)
        at = pl.ds(pl.multiple_of((yd * X + 2 * xd + cd) * T, T), T)
        return pltpu.make_async_copy(xall.at[at], xs.at[slot], xsem.at[slot])

    def xstart(s, slot):
        a, b = offs(s // 2)
        kk = lax.rem(s, 2)
        mine = (a + b + kk) == 0

        @pl.when(kk == 1)
        def _():
            yd, xd, cd = dest(s)
            at = pl.ds(pl.multiple_of((yd * X + 2 * xd + cd) * T, T), T)
            arrive(xall.at[at], dsem.at[a * 4 + b])

        @pl.when(mine)
        def _():
            pltpu.make_async_copy(x, xs.at[slot], xsem.at[slot]).start()

        @pl.when(jnp.logical_not(mine))
        def _():
            xcopy(s, slot).start()

    def send_a(s):
        yd, xd, cd = dest(s)
        return pltpu.make_async_remote_copy(
            src_ref=block(stage.at[0], yd * X + 2 * xd + cd), dst_ref=block(recv.at[0], at_a(yd, mx)),
            send_sem=ssem.at[0, s], recv_sem=rsem.at[0, s],
            device_id={'outer': mo, 'expert': 2 * xd + cd}, device_id_type=MESH)

    def send_b(s):
        yd, xd, cd = dest(s)
        return pltpu.make_async_remote_copy(
            src_ref=block(stage.at[1], yd * X + 2 * xd + cd), dst_ref=block(recv.at[1], at_b(xd, mo, core)),
            send_sem=ssem.at[1, s], recv_sem=rsem.at[1, s],
            device_id={'outer': yd, 'expert': 2 * mc + cd}, device_id_type=MESH)

    def away(s):
        a, b = offs(s // 2)
        k = lax.rem(s, 2)
        return b + k > 0, a + k > 0

    def experts(w1v, w3v, w2v, xt):
        def wcopies(e):
            return (pltpu.make_async_copy(w1.at[e], w1v.at[e], wsem.at[0, e]),
                    pltpu.make_async_copy(w3.at[e], w3v.at[e], wsem.at[1, e]),
                    pltpu.make_async_copy(w2.at[e], w2v.at[e], wsem.at[2, e]))

        pl.semaphore_wait(bar, n - 1)
        step = T // 2
        for h in (0, 1):
            own = x.at[pl.ds(h * step, step)]
            for d in (1, 3):
                relay(h, (0, 0), 0, d, None, own)
        for h in (0, 1):
            own = x.at[pl.ds(h * step, step)]
            for d in (1, 3):
                relay(h, (0, 0), 1, d, None, own)
        for h in (0, 1):
            share(h, (0, 0), x.at[pl.ds(h * step, step)])

        def tell(d, _):
            t = lax.rem(me + d, n)
            to, tx = t // X, lax.rem(t, X)
            pltpu.make_async_remote_copy(
                src_ref=pk.at[0, to, tx], dst_ref=tab_in.at[me], send_sem=tsem.at[0], recv_sem=tsem.at[1],
                device_id={'outer': to, 'expert': tx}, device_id_type=MESH).start()
            return 0

        lax.fori_loop(1, n, tell, 0)
        pltpu.make_async_copy(pk.at[0, mo, mx], tab_in.at[me], tsem2.at[0, 0]).start()
        for d in range(4):
            yo, xo = lax.rem(mo + d, O), lax.rem(mc + d, W)
            if d == 0:
                pltpu.make_async_copy(pk.at[:, mo], pk_a.at[mo], tsem2.at[1, 0]).start()
                pltpu.make_async_copy(pk.at[:, :, pl.ds(2 * mc, 2)], pk_b.at[mc], tsem2.at[2, 0]).start()
            else:
                tsend(0, d).start()
                tsend(1, d).start()
        for e in range(el):
            for cp in wcopies(e):
                cp.start()
        tok = lax.broadcasted_iota(jnp.int32, (T, B), 0).astype(F32)

        for h in (0, 1):
            for u in (1, 3):
                event(h, (u, 0))
        for h in (0, 1):
            for v in (1, 3):
                event(h, (0, v))
        pltpu.make_async_copy(pk.at[0, mo, mx], tab_in.at[me], tsem2.at[0, 0]).wait()
        allrows = pltpu.make_async_remote_copy(
            src_ref=tab_in.at[pl.ds(0, n - 1)], dst_ref=tab_in.at[pl.ds(0, n - 1)], send_sem=tsem.at[0],
            recv_sem=tsem.at[1], device_id=other(), device_id_type=MESH)
        allrows.wait_recv()

        diag = [(h, (u, v)) for u in (1, 3) for v in (1, 3) for h in (0, 1)]
        plan = {0: [(0, (2, 0))], 1: [(1, (2, 0))], 3: [(0, (0, 2))], 4: [(1, (0, 2))],
                5: diag[0:2], 6: diag[2:4], 8: diag[4:6], 9: diag[6:8],
                12: [(0, (2, 1)), (1, (2, 1))], 13: [(0, (2, 3)), (1, (2, 3))],
                15: [(0, (1, 2)), (1, (1, 2))], 16: [(0, (3, 2)), (1, (3, 2))],
                20: [(0, (2, 2)), (1, (2, 2))]}

        xstart(0, 0)

        def group(g, _):
            def pick(j, _):
                s = g * G + j
                slot = lax.rem(s, 2)

                @pl.when(j + 1 < G)
                def _():
                    xstart(s + 1, 1 - slot)
                xcopy(s, slot).wait()
                yd, xd, cd = dest(s)
                row = tab_in[yd * X + 2 * xd + cd]
                hot = jnp.where(tok == row, 1.0, 0.0).astype(BF16)
                at = pl.ds(pl.multiple_of(j * C, C), C)
                for c0 in range(0, D, NT):
                    r = lax.dot_general(hot, xs[slot, :, c0:c0 + NT], (((0,), (0,)), ((), ())),
                                        preferred_element_type=F32).astype(BF16)
                    for e in range(el):
                        xt[e, at, c0:c0 + NT] = r[e * C:(e + 1) * C]
                return 0

            lax.fori_loop(0, G, pick, 0)

            def odrain(hh):
                for v in range(2):
                    pltpu.make_async_copy(ob.at[hh, :, pl.ds(v * H, H)], stage.at[v, pl.ds(0, half)],
                                          osem.at[hh, v]).wait()

            def ffn(e, _):
                hh = lax.rem(e, 2)

                @pl.when(g == 0)
                def _():
                    for cp in wcopies(e):
                        cp.wait()
                xr = xt[e]
                a = jnp.dot(xr, w1v[e], preferred_element_type=F32)
                b = jnp.dot(xr, w3v[e], preferred_element_type=F32)
                h = (jax.nn.silu(a) * b).astype(BF16)

                @pl.when(e >= 2)
                def _():
                    odrain(hh)
                for c0 in range(0, D, NT):
                    ob[hh, :, c0:c0 + NT] = jnp.dot(h, w2v[e, :, c0:c0 + NT],
                                                    preferred_element_type=F32).astype(BF16)
                for jj in range(G):
                    yd, xd, cd = dest(g * G + jj)
                    at = pl.ds(pl.multiple_of((yd * X + 2 * xd + cd) * B + e * C, C), C)
                    for v in range(2):
                        pltpu.make_async_copy(ob.at[hh, pl.ds(jj * C, C), pl.ds(v * H, H)],
                                              stage.at[v, at], osem.at[hh, v]).start()
                for t, todo in plan.items():
                    @pl.when(g * el + e == t)
                    def _(todo=todo):
                        for h, off in todo:
                            event(h, off)

                @pl.when((e == el - 2) & (g + 1 < NG))
                def _():
                    xstart((g + 1) * G, 0)
                return 0

            lax.fori_loop(0, el, ffn, 0)
            for hh in range(2):
                odrain(hh)

            def go(j, _):
                s = g * G + j
                far_a, far_b = away(s)

                @pl.when(far_a)
                def _():
                    send_a(s).start()

                @pl.when(far_b)
                def _():
                    send_b(s).start()
                return 0

            lax.fori_loop(0, G, go, 0)
            return 0

        lax.fori_loop(0, NG, group, 0)

    def tsend(v, d):
        yo, xo = lax.rem(mo + d, O), lax.rem(mc + d, W)
        if v == 0:
            src, dst, to = pk.at[:, yo], pk_a.at[mo], {'outer': yo, 'expert': mx}
        else:
            src, dst, to = pk.at[:, :, pl.ds(2 * xo, 2)], pk_b.at[mc], {'outer': mo, 'expert': 2 * xo + core}
        return pltpu.make_async_remote_copy(src_ref=src, dst_ref=dst, send_sem=tsem2.at[1 + v, d],
                                            recv_sem=tsem2.at[3 + v, d], device_id=to, device_id_type=MESH)

    pl.run_scoped(experts, pltpu.VMEM((el, D, FF), BF16), pltpu.VMEM((el, D, FF), BF16),
                  pltpu.VMEM((el, FF, D), BF16), pltpu.VMEM((el, half, D), BF16))

    pltpu.make_async_copy(pk.at[:, mo], pk_a.at[mo], tsem2.at[1, 0]).wait()
    pltpu.make_async_copy(pk.at[:, :, pl.ds(2 * mc, 2)], pk_b.at[mc], tsem2.at[2, 0]).wait()
    for d in range(1, 4):
        tsend(0, d).wait()
        tsend(1, d).wait()

    def combine(pa, pb):
        pa[...] = jnp.zeros_like(pa)
        pb[...] = jnp.zeros_like(pb)
        tokf = lax.broadcasted_iota(jnp.int32, (T, 2 * B), 0).astype(F32)

        def origins(p):
            a, b = offs(p)
            return a, b, lax.rem(mo - a + O, O), lax.rem(mc - b + W, W)

        def fetch(p, slot):
            a, b, sy, sx = origins(p)
            yd, xd = lax.rem(mo + a, O), lax.rem(mc + b, W)
            for k in range(2):
                s = 2 * p + k
                c = lax.rem(core + k, 2)
                at = pl.ds(pl.multiple_of(c * B, B), B)
                for v in range(2):
                    if v == 0:
                        src, own = block(recv.at[0], at_a(yd, 2 * sx + c)), block(stage.at[0], yd * X + 2 * mc + core)
                    else:
                        src, own = block(recv.at[1], at_b(xd, sy, c)), block(stage.at[1], mo * X + 2 * xd + core)
                    far = (b if v == 0 else a) > 0

                    def bring(ref, v=v, at=at):
                        pltpu.make_async_copy(ref, xs.at[slot, at, pl.ds(v * H, H)], xsem.at[slot]).start()

                    def take(src=src, v=v, s=s, bring=bring):
                        pltpu.make_async_remote_copy(
                            src_ref=src, dst_ref=src, send_sem=ssem.at[v, s],
                            recv_sem=rsem.at[v, s],
                            device_id={'outer': mo, 'expert': lax.rem(mx + 1, X)},
                            device_id_type=MESH).wait_recv()
                        bring(src)
                    if k == 1:
                        take()
                    else:
                        pl.when(far)(take)
                        pl.when(jnp.logical_not(far))(functools.partial(bring, own))

        def psend(v, d):
            if v == 0:
                src, to = pa.at[d], {'outer': lax.rem(mo + d, O), 'expert': mx}
            else:
                src, to = pb.at[d], {'outer': mo, 'expert': 2 * lax.rem(mc + d, W) + core}
            return pltpu.make_async_remote_copy(
                src_ref=src, dst_ref=part.at[v, d - 1], send_sem=pssem.at[v, d - 1],
                recv_sem=prsem.at[v, d - 1], device_id=to, device_id_type=MESH)

        fetch(0, 0)

        def weights(ref, d, r0):
            out = []
            rows = [ref[(d, 0) + r0(c)] for c in range(2)]
            gs = [ref[(d, 1) + r0(c)] for c in range(2)]
            w = jnp.where(tokf == jnp.concatenate(rows, axis=1), jnp.concatenate(gs, axis=1), 0.0)
            hi = w.astype(BF16)
            r = w - hi.astype(F32)
            mid = r.astype(BF16)
            return hi, mid, (r - mid.astype(F32)).astype(BF16)

        def comb(p, _):
            slot = lax.rem(p, 2)

            @pl.when(p + 1 < n // 2)
            def _():
                fetch(p + 1, 1 - slot)
            a, b, sy, sx = origins(p)
            wa = weights(pk_a, lax.rem(mo + a, O), lambda c: (2 * sx + c,))
            wb = weights(pk_b, lax.rem(mc + b, W), lambda c: (sy, c))
            pltpu.make_async_copy(xall.at[pl.ds(0, T)], xs.at[slot], xsem.at[slot]).wait()
            for acc, d, ws, base in ((pa, a, wa, 0), (pb, b, wb, H)):
                for c0 in range(0, H, NT):
                    rr = xs[slot, :, base + c0:base + c0 + NT]
                    acc[d, :, c0:c0 + NT] += (jnp.dot(ws[0], rr, preferred_element_type=F32)
                                              + jnp.dot(ws[1], rr, preferred_element_type=F32)
                                              + jnp.dot(ws[2], rr, preferred_element_type=F32))
            for last, v, ds in ((11, 0, (1, 3)), (13, 1, (1, 3)), (15, 0, (2,)), (15, 1, (2,))):
                @pl.when(p == last)
                def _(v=v, ds=ds):
                    for d in ds:
                        psend(v, d).start()
            return 0

        lax.fori_loop(0, n // 2, comb, 0)

        def sent(s, _):
            far_a, far_b = away(s)

            @pl.when(far_a)
            def _():
                send_a(s).wait_send()

            @pl.when(far_b)
            def _():
                send_b(s).wait_send()
            return 0

        lax.fori_loop(0, n, sent, 0)

        def wsend(ref, sem):
            pltpu.make_async_remote_copy(src_ref=ref, dst_ref=ref, send_sem=sem, recv_sem=tsem.at[1],
                                         device_id=other(), device_id_type=MESH).wait_send()

        def gone(i, _):
            wsend(xall.at[pl.ds(0, T // 2)], gsem.at[i])
            return 0

        lax.fori_loop(0, len(FULL), gone, 0)

        def gonep(i, _):
            wsend(xall.at[pl.ds(0, T // 4)], gpsem.at[i])
            return 0

        lax.fori_loop(0, len(PIECE), gonep, 0)

        def goneh(i, _):
            wsend(xall.at[pl.ds(0, T // 2)], hsem.at[i])
            return 0

        lax.fori_loop(0, n, goneh, 0)
        wsend(tab_in.at[pl.ds(0, n - 1)], tsem.at[0])

        accs = (pa, pb)
        for d in (1, 3, 2):
            for v in range(2):
                psend(v, d).wait()
                pltpu.make_async_copy(part.at[v, d - 1], accs[v].at[d], prsem.at[v, d - 1]).start()
            for v in range(2):
                pltpu.make_async_copy(part.at[v, d - 1], accs[v].at[d], prsem.at[v, d - 1]).wait()
                if d != 2:
                    accs[v][0] += accs[v][d]
        for v in range(2):
            for hh in range(T // half):
                rows = slice(hh * half, (hh + 1) * half)
                ob[hh, :, v * H:(v + 1) * H] = (accs[v][0, rows] + accs[v][2, rows]).astype(BF16)
        cps = [pltpu.make_async_copy(ob.at[hh], y.at[pl.ds(hh * half, half)], osem.at[hh, 0])
               for hh in range(T // half)]
        for cp in cps:
            cp.start()
        for cp in cps:
            cp.wait()

    pl.run_scoped(combine, pltpu.VMEM((O, T, H), F32), pltpu.VMEM((W, T, H), F32))


def solution(mesh):
    O = mesh.shape['outer']
    X = mesh.shape['expert']
    n = O * X
    tok = P(('data', 'outer', 'expert'), None)
    wsp = P(('outer', 'expert'), None, None)

    def local(x, wr, idx, w1, w3, w2):
        T, D = x.shape
        k = idx.shape[1]
        E = wr.shape[1]
        el, _, FF = w1.shape
        C = 2 * T * k // E
        B = el * C
        g = _gate(x, wr, idx)
        tab, gs = _tables(idx, g, E, C)
        pk = jnp.stack((tab.astype(F32), gs)).reshape(2, O, X, 1, B)
        anyspec = pl.BlockSpec(memory_space=pl.ANY)
        y = pl.pallas_call(
            functools.partial(_kernel, O, X, el, C),
            out_shape=(jax.ShapeDtypeStruct((T, D), BF16),
                       jax.ShapeDtypeStruct((n * T, D), BF16),
                       jax.ShapeDtypeStruct((2, n * B, D // 2), BF16),
                       jax.ShapeDtypeStruct((2, n * B, D // 2), BF16),
                       jax.ShapeDtypeStruct((2, O - 1, T, D // 2), F32)),
            in_specs=[anyspec] * 5,
            out_specs=(anyspec,) * 5,
            scratch_shapes=[
                pltpu.VMEM((2, T, D), BF16),
                pltpu.VMEM((2, 4 * C, D), BF16),
                pltpu.VMEM((n, 1, B), F32),
                pltpu.VMEM((O, 2, X, 1, B), F32),
                pltpu.VMEM((X // 2, 2, O, 2, 1, B), F32),
                pltpu.SemaphoreType.DMA((3, el)),
                pltpu.SemaphoreType.DMA((2,)),
                pltpu.SemaphoreType.DMA((2, 2)),
                pltpu.SemaphoreType.DMA((2, n)),
                pltpu.SemaphoreType.DMA((2, n)),
                pltpu.SemaphoreType.DMA((2, O - 1)),
                pltpu.SemaphoreType.DMA((2, O - 1)),
                pltpu.SemaphoreType.DMA((32,)),
                pltpu.SemaphoreType.DMA((64,)),
                pltpu.SemaphoreType.DMA((32,)),
                pltpu.SemaphoreType.DMA((32,)),
                pltpu.SemaphoreType.DMA((16,)),
                pltpu.SemaphoreType.DMA((32,)),
                pltpu.SemaphoreType.DMA((2,)),
                pltpu.SemaphoreType.DMA((5, 4)),
            ],
            compiler_params=pltpu.CompilerParams(
                collective_id=0, has_side_effects=True, vmem_limit_bytes=67043328),
        )(x, pk, w1, w3, w2)
        return y[0]

    return jax.shard_map(local, mesh=mesh, in_specs=(tok, P(None, None), tok, wsp, wsp, wsp), out_specs=tok, check_vma=False)
```

time: 570 us -> 469 us (0.82)
  the two profiles are of different devices: /device:TPU:121 before, /device:TPU:97 now
where the time goes in v3:
time: 469 us; the launch traced here: 468 us
  Pallas kernels  457 us (97%)
    pallas_call x1, Pallas kernels, local(): pl.pallas_call(functools.partial(_kernel, O, X, el, C), out_shape=(jax.Sh...  457 us

profile of v3, /device:TPU:97, one launch (start us, length us, event | category | flops | bytes accessed | tf_op | source)
XLA Modules:
  0.0 467.8 jit_solution(10522685054199264839)
XLA Ops:
  0.0 0.0 copy-start
  0.1 2.4 fusion.28
  2.4 0.0 copy-done
  2.5 0.7 convert_reduce_fusion
  3.2 0.3 fusion.10
  3.5 1.9 select_reduce_fusion.1
  5.5 0.1 iota_compare_fusion.1
  5.6 1.1 fusion.6
  6.8 0.1 copy.9
  6.9 0.1 stack.27
  7.0 0.1 copy.10
  7.1 0.1 stack.28
  7.2 0.7 pad_maximum_fusion.pk
  7.9 456.8 %shard_map.64 = (bf16[512,2048]{1,0:T(8,128)(2,1)}, bf16[16384,2048]{1,0:T(8,128)(2,1)}, bf16[2,8192,1024]{2,1,0:T(8,128)(2,1)}, bf16[2,8192,1024]{2,1,0:T(8,128)(2,1)}, f32[2,3,512,1024]{3,2,1,0:T(8,128)}) custom-call(bf16[512,2048]{1,0:T(8,128)(2,1)} %x.1, f32[2,4,8,1,256]{4,3,2,1,0:T(1,128)} %pad_maximum_fusion.pk, bf16[4,2048,768]{2,1,0:T(8,128)(2,1)} %w1.1, ...), custom_call_target="tpu_custom_call" | custom-call | tf_op jit(solution)/shard_map/pallas_call | solution.py:561
  464.7 3.2 copy.20
  (11 shorter events, 0.1 us)
Async XLA Ops:
  0.0 2.4 copy-start

commit v4 on v3

--- a/solution.py
+++ b/solution.py
@@ -46,6 +46,10 @@
 
 ORDER = ((0, 1), (0, 3), (1, 0), (3, 0), (0, 0), (0, 2), (1, 1), (3, 3),
          (1, 3), (3, 1), (1, 2), (3, 2), (2, 1), (2, 3), (2, 0), (2, 2))
+NEAR = (1, 3)
+EARLY, MID, LATE = range(3)
+HERE = (0, 0)
+TIMES = (0, 3, 5, 6, 8, 9, 12, 13, 15, 16, 20)
 
 
 def _lut(vals, i):
@@ -73,15 +77,14 @@
 def _numbered():
     full, piece = {}, {}
     for h in range(2):
-        for d in (1, 3):
+        for d in NEAR:
             for axis in range(2):
-                full[(h, (0, 0), axis, d)] = len(full)
-        for u in range(4):
-            for v in range(4):
-                if (u, v) != (0, 0):
-                    for axis, d, part in _relays(h, (u, v)):
-                        table = full if part is None else piece
-                        table[(h, (u, v), axis, d)] = len(table)
+                full[(h, HERE, axis, d)] = len(full)
+        for off in ORDER:
+            if off != HERE:
+                for axis, d, part in _relays(h, off):
+                    table = full if part is None else piece
+                    table[(h, off, axis, d)] = len(table)
     return full, piece
 
 
@@ -89,7 +92,7 @@
 
 
 def _kernel(O, X, el, C, x, pk, w1, w3, w2, y, xall, stage, recv, part,
-            xs, ob, tab_in, pk_a, pk_b, wsem, xsem, osem, ssem, rsem, pssem, prsem,
+            xs, ob, tab_in, pk_a, pk_b, mid, wsem, xsem, osem, ssem, rsem, pssem, prsem, psem,
             bsem, bpsem, gsem, gpsem, dsem, hsem, tsem, tsem2):
     n = O * X
     W = X // 2
@@ -238,16 +241,13 @@
 
         pl.semaphore_wait(bar, n - 1)
         step = T // 2
-        for h in (0, 1):
-            own = x.at[pl.ds(h * step, step)]
-            for d in (1, 3):
-                relay(h, (0, 0), 0, d, None, own)
-        for h in (0, 1):
-            own = x.at[pl.ds(h * step, step)]
-            for d in (1, 3):
-                relay(h, (0, 0), 1, d, None, own)
-        for h in (0, 1):
-            share(h, (0, 0), x.at[pl.ds(h * step, step)])
+        own = [x.at[pl.ds(h * step, step)] for h in range(2)]
+        for axis in range(2):
+            for h in range(2):
+                for d in NEAR:
+                    relay(h, HERE, axis, d, None, own[h])
+        for h in range(2):
+            share(h, HERE, own[h])
 
         def tell(d, _):
             t = lax.rem(me + d, n)
@@ -272,24 +272,19 @@
                 cp.start()
         tok = lax.broadcasted_iota(jnp.int32, (T, B), 0).astype(F32)
 
-        for h in (0, 1):
-            for u in (1, 3):
-                event(h, (u, 0))
-        for h in (0, 1):
-            for v in (1, 3):
-                event(h, (0, v))
+        for axis in range(2):
+            for h in range(2):
+                for d in NEAR:
+                    event(h, (0, d) if axis else (d, 0))
         pltpu.make_async_copy(pk.at[0, mo, mx], tab_in.at[me], tsem2.at[0, 0]).wait()
         allrows = pltpu.make_async_remote_copy(
             src_ref=tab_in.at[pl.ds(0, n - 1)], dst_ref=tab_in.at[pl.ds(0, n - 1)], send_sem=tsem.at[0],
             recv_sem=tsem.at[1], device_id=other(), device_id_type=MESH)
         allrows.wait_recv()
 
-        diag = [(h, (u, v)) for u in (1, 3) for v in (1, 3) for h in (0, 1)]
-        plan = {0: [(0, (2, 0))], 1: [(1, (2, 0))], 3: [(0, (0, 2))], 4: [(1, (0, 2))],
-                5: diag[0:2], 6: diag[2:4], 8: diag[4:6], 9: diag[6:8],
-                12: [(0, (2, 1)), (1, (2, 1))], 13: [(0, (2, 3)), (1, (2, 3))],
-                15: [(0, (1, 2)), (1, (1, 2))], 16: [(0, (3, 2)), (1, (3, 2))],
-                20: [(0, (2, 2)), (1, (2, 2))]}
+        later = [(2, 0), (0, 2)] + [(u, v) for u in NEAR for v in NEAR]
+        later += [(2, v) for v in NEAR] + [(u, 2) for u in NEAR] + [(2, 2)]
+        plan = dict(zip(TIMES, later))
 
         xstart(0, 0)
 
@@ -347,8 +342,8 @@
                 for t, todo in plan.items():
                     @pl.when(g * el + e == t)
                     def _(todo=todo):
-                        for h, off in todo:
-                            event(h, off)
+                        for h in range(2):
+                            event(h, todo)
 
                 @pl.when((e == el - 2) & (g + 1 < NG))
                 def _():
@@ -434,19 +429,32 @@
                         pl.when(far)(take)
                         pl.when(jnp.logical_not(far))(functools.partial(bring, own))
 
-        def psend(v, d):
+        accs = (pa, pb)
+        hr = T // 2
+        pairs = [(v, r) for v in range(2) for r in range(2)]
+
+        def late(r):
+            return pl.ds(r * hr, hr)
+
+        def psend(kind, v, r):
+            d = NEAR[r]
+            if kind == EARLY:
+                src, dst = accs[v].at[d, late(1 - r)], part.at[v, r, late(1 - r)]
+            elif kind == MID:
+                src, dst = accs[v].at[2, late(r)], mid.at[v, r]
+            else:
+                src, dst = accs[v].at[d, late(r)], part.at[v, r, late(r)]
             if v == 0:
-                src, to = pa.at[d], {'outer': lax.rem(mo + d, O), 'expert': mx}
+                to = {'outer': lax.rem(mo + d, O), 'expert': mx}
             else:
-                src, to = pb.at[d], {'outer': mo, 'expert': 2 * lax.rem(mc + d, W) + core}
+                to = {'outer': mo, 'expert': 2 * lax.rem(mc + d, W) + core}
             return pltpu.make_async_remote_copy(
-                src_ref=src, dst_ref=part.at[v, d - 1], send_sem=pssem.at[v, d - 1],
-                recv_sem=prsem.at[v, d - 1], device_id=to, device_id_type=MESH)
+                src_ref=src, dst_ref=dst, send_sem=pssem.at[kind, v, r], recv_sem=prsem.at[kind, v, r],
+                device_id=to, device_id_type=MESH)
 
         fetch(0, 0)
 
         def weights(ref, d, r0):
-            out = []
             rows = [ref[(d, 0) + r0(c)] for c in range(2)]
             gs = [ref[(d, 1) + r0(c)] for c in range(2)]
             w = jnp.where(tokf == jnp.concatenate(rows, axis=1), jnp.concatenate(gs, axis=1), 0.0)
@@ -471,14 +479,28 @@
                     acc[d, :, c0:c0 + NT] += (jnp.dot(ws[0], rr, preferred_element_type=F32)
                                               + jnp.dot(ws[1], rr, preferred_element_type=F32)
                                               + jnp.dot(ws[2], rr, preferred_element_type=F32))
-            for last, v, ds in ((11, 0, (1, 3)), (13, 1, (1, 3)), (15, 0, (2,)), (15, 1, (2,))):
+            for last, kind, sides in ((11, EARLY, pairs[:2]), (13, EARLY, pairs[2:]), (15, MID, pairs)):
                 @pl.when(p == last)
-                def _(v=v, ds=ds):
-                    for d in ds:
-                        psend(v, d).start()
+                def _(kind=kind, sides=sides):
+                    for v, r in sides:
+                        psend(kind, v, r).start()
             return 0
 
         lax.fori_loop(0, n // 2, comb, 0)
+
+        def land(v, r, half_):
+            return pltpu.make_async_copy(part.at[v, r, late(half_)], accs[v].at[NEAR[r], late(half_)], psem.at[v, r])
+
+        for v, r in pairs:
+            psend(EARLY, v, r).wait()
+            land(v, r, 1 - r).start()
+        for v, r in pairs:
+            land(v, r, 1 - r).wait()
+            accs[v][0, late(1 - r)] += accs[v][NEAR[r], late(1 - r)]
+        for v, r in pairs:
+            psend(MID, v, r).wait()
+            accs[v][NEAR[r], late(r)] += mid[v, r]
+            psend(LATE, v, r).start()
 
         def sent(s, _):
             far_a, far_b = away(s)
@@ -517,19 +539,12 @@
         lax.fori_loop(0, n, goneh, 0)
         wsend(tab_in.at[pl.ds(0, n - 1)], tsem.at[0])
 
-        accs = (pa, pb)
-        for d in (1, 3, 2):
-            for v in range(2):
-                psend(v, d).wait()
-                pltpu.make_async_copy(part.at[v, d - 1], accs[v].at[d], prsem.at[v, d - 1]).start()
-            for v in range(2):
-                pltpu.make_async_copy(part.at[v, d - 1], accs[v].at[d], prsem.at[v, d - 1]).wait()
-                if d != 2:
-                    accs[v][0] += accs[v][d]
-        for v in range(2):
-            for hh in range(T // half):
-                rows = slice(hh * half, (hh + 1) * half)
-                ob[hh, :, v * H:(v + 1) * H] = (accs[v][0, rows] + accs[v][2, rows]).astype(BF16)
+        for v, r in pairs:
+            psend(LATE, v, r).wait()
+            land(v, r, r).start()
+        for v, r in pairs:
+            land(v, r, r).wait()
+            ob[r, :, v * H:(v + 1) * H] = (accs[v][0, late(r)] + accs[v][NEAR[r], late(r)]).astype(BF16)
         cps = [pltpu.make_async_copy(ob.at[hh], y.at[pl.ds(hh * half, half)], osem.at[hh, 0])
                for hh in range(T // half)]
         for cp in cps:
@@ -564,7 +579,7 @@
                        jax.ShapeDtypeStruct((n * T, D), BF16),
                        jax.ShapeDtypeStruct((2, n * B, D // 2), BF16),
                        jax.ShapeDtypeStruct((2, n * B, D // 2), BF16),
-                       jax.ShapeDtypeStruct((2, O - 1, T, D // 2), F32)),
+                       jax.ShapeDtypeStruct((2, 2, T, D // 2), F32)),
             in_specs=[anyspec] * 5,
             out_specs=(anyspec,) * 5,
             scratch_shapes=[
@@ -573,13 +588,15 @@
                 pltpu.VMEM((n, 1, B), F32),
                 pltpu.VMEM((O, 2, X, 1, B), F32),
                 pltpu.VMEM((X // 2, 2, O, 2, 1, B), F32),
+                pltpu.VMEM((2, 2, T // 2, D // 2), F32),
                 pltpu.SemaphoreType.DMA((3, el)),
                 pltpu.SemaphoreType.DMA((2,)),
                 pltpu.SemaphoreType.DMA((2, 2)),
                 pltpu.SemaphoreType.DMA((2, n)),
                 pltpu.SemaphoreType.DMA((2, n)),
-                pltpu.SemaphoreType.DMA((2, O - 1)),
-                pltpu.SemaphoreType.DMA((2, O - 1)),
+                pltpu.SemaphoreType.DMA((3, 2, 2)),
+                pltpu.SemaphoreType.DMA((3, 2, 2)),
+                pltpu.SemaphoreType.DMA((2, 2)),
                 pltpu.SemaphoreType.DMA((32,)),
                 pltpu.SemaphoreType.DMA((64,)),
                 pltpu.SemaphoreType.DMA((32,)),

time: 469 us -> 448 us (0.955)
  Pallas kernels: 457 us -> 437 us
    pallas_call x1, Pallas kernels: 457 us -> 437 us  [local(): pl.pallas_call(functools.partial(_kernel, O, X, el, C), out_shape=(jax.Sh...]
where the time goes in v4:
time: 448 us
  Pallas kernels  437 us (98%)
    pallas_call x1, Pallas kernels, local(): pl.pallas_call(functools.partial(_kernel, O, X, el, C), out_shape=(jax.Sh...  437 us

profile of v4, /device:TPU:97, one launch (start us, length us, event | category | flops | bytes accessed | tf_op | source)
XLA Modules:
  0.0 447.7 jit_solution(3643335890202971650)
XLA Ops:
  0.0 0.0 copy-start
  0.1 2.4 fusion.28
  2.4 0.0 copy-done
  2.4 0.7 convert_reduce_fusion
  3.2 0.3 fusion.10
  3.5 1.9 select_reduce_fusion.1
  5.5 0.1 iota_compare_fusion.1
  5.6 1.1 fusion.6
  6.8 0.1 copy.9
  6.9 0.1 stack.27
  7.0 0.1 copy.10
  7.1 0.1 stack.28
  7.2 0.7 pad_maximum_fusion.pk
  7.9 436.7 %shard_map.64 = (bf16[512,2048]{1,0:T(8,128)(2,1)}, bf16[16384,2048]{1,0:T(8,128)(2,1)}, bf16[2,8192,1024]{2,1,0:T(8,128)(2,1)}, bf16[2,8192,1024]{2,1,0:T(8,128)(2,1)}, f32[2,2,512,1024]{3,2,1,0:T(8,128)}) custom-call(bf16[512,2048]{1,0:T(8,128)(2,1)} %x.1, f32[2,4,8,1,256]{4,3,2,1,0:T(1,128)} %pad_maximum_fusion.pk, bf16[4,2048,768]{2,1,0:T(8,128)(2,1)} %w1.1, ...), custom_call_target="tpu_custom_call" | custom-call | tf_op jit(solution)/shard_map/pallas_call | solution.py:576
  444.6 3.2 copy.20
  (11 shorter events, 0.1 us)
Async XLA Ops:
  0.0 2.4 copy-start

commit v5 on v4

--- a/solution.py
+++ b/solution.py
@@ -12,36 +12,46 @@
 BF16 = jnp.bfloat16
 
 
-def _gate(x, wr, idx):
-    logits = jnp.dot(x, wr, preferred_element_type=F32)
-    oh = idx[:, :, None] == jnp.arange(wr.shape[1], dtype=idx.dtype)
-    return jax.nn.softmax(jnp.sum(jnp.where(oh, logits[:, None, :], 0.0), axis=-1), axis=-1)
-
-
-def _parts(w):
-    hi = lax.reduce_precision(w, 8, 7)
-    r = w - hi
-    mid = lax.reduce_precision(r, 8, 7)
-    return hi, mid, r - mid
-
-
-def _tables(idx, g, E, C):
-    t, k = idx.shape
-    oh = idx[:, :, None] == jnp.arange(E, dtype=idx.dtype)
-    m = jnp.sum(oh, axis=1, dtype=jnp.int32).astype(BF16)
-    pos = jnp.arange(t, dtype=jnp.int32)
-    tri = (pos[None, :] < pos[:, None]).astype(BF16)
-    cnt = jnp.dot(tri, m, preferred_element_type=F32)
-    r = jnp.sum(jnp.where(oh, cnt[:, None, :], 0.0), axis=-1)
-    ohr = r[:, :, None] == jnp.arange(C, dtype=F32)
-    one = jnp.ones((t, k), F32)
-    lo = (pos % 256).astype(F32)[:, None] * one
-    hi = (pos // 256).astype(F32)[:, None] * one
-    vals = jnp.stack((one, hi, lo) + _parts(g), axis=-1)
-    rhs = jnp.where(ohr[:, :, None, :], vals[..., None], 0.0).astype(BF16)
-    res = jnp.einsum('tje,tjic->iec', oh.astype(BF16), rhs, preferred_element_type=F32)
-    tab = jnp.where(res[0] > 0.5, res[1] * 256.0 + res[2], -1.0).astype(jnp.int32)
-    return tab, (res[3] + res[4]) + res[5]
+def _split(w):
+    hi = w.astype(BF16)
+    r = w - hi.astype(F32)
+    mid = r.astype(BF16)
+    return hi, mid, (r - mid.astype(F32)).astype(BF16)
+
+
+def _tables(xv, wr, idx, C):
+    T, k = idx.shape
+    E = wr.shape[1]
+    logits = jnp.dot(xv, wr, preferred_element_type=F32)
+    lane = lax.broadcasted_iota(jnp.int32, (T, E), 1)
+    hits = [idx[:, j:j + 1] == lane for j in range(k)]
+
+    def take(table):
+        return [jnp.sum(jnp.where(h, table, 0.0), axis=1, keepdims=True) for h in hits]
+
+    at = take(logits)
+    top = functools.reduce(jnp.maximum, at)
+    ex = [jnp.exp(v - top) for v in at]
+    tot = functools.reduce(jnp.add, ex)
+    ones = [jnp.where(h, 1.0, 0.0) for h in hits]
+    many = functools.reduce(jnp.add, ones).astype(BF16)
+    tri = lax.broadcasted_iota(jnp.int32, (T, T), 1) < lax.broadcasted_iota(jnp.int32, (T, T), 0)
+    rank = take(jnp.dot(jnp.where(tri, 1.0, 0.0).astype(BF16), many, preferred_element_type=F32))
+    slot = lax.rem(lane, C).astype(F32)
+    left = lane < C
+    tok = lax.broadcasted_iota(jnp.int32, (T, 1), 0) + 1
+    lo = lax.rem(tok, T // 2).astype(F32)
+    hi = (tok // (T // 2)).astype(F32)
+    res = [0.0] * 3
+    for j in range(k):
+        g = [v.astype(F32) for v in _split(ex[j] / tot)]
+        hot = ones[j].astype(BF16)
+        here = rank[j] == slot
+        for i, (u, v) in enumerate(((hi, lo), (g[0], g[1]), (g[2], g[2]))):
+            val = jnp.where(here, jnp.where(left, u, v), 0.0).astype(BF16)
+            res[i] += lax.dot_general(hot, val, (((0,), (0,)), ((), ())), preferred_element_type=F32)
+    tab = res[0][:, :C] * (T // 2) + res[0][:, C:2 * C] - 1.0
+    return tab, (res[1][:, :C] + res[1][:, C:2 * C]) + res[2][:, :C]
 
 
 ORDER = ((0, 1), (0, 3), (1, 0), (3, 0), (0, 0), (0, 2), (1, 1), (3, 3),
@@ -91,8 +101,8 @@
 FULL, PIECE = _numbered()
 
 
-def _kernel(O, X, el, C, x, pk, w1, w3, w2, y, xall, stage, recv, part,
-            xs, ob, tab_in, pk_a, pk_b, mid, wsem, xsem, osem, ssem, rsem, pssem, prsem, psem,
+def _kernel(O, X, el, C, x, wr, idx, w1, w3, w2, y, xall, stage, recv, part,
+            xs, ob, pk, flat, tab_in, pk_a, pk_b, mid, wsem, xsem, osem, ssem, rsem, pssem, prsem, psem,
             bsem, bpsem, gsem, gpsem, dsem, hsem, tsem, tsem2):
     n = O * X
     W = X // 2
@@ -239,13 +249,29 @@
                     pltpu.make_async_copy(w3.at[e], w3v.at[e], wsem.at[1, e]),
                     pltpu.make_async_copy(w2.at[e], w2v.at[e], wsem.at[2, e]))
 
+        pltpu.make_async_copy(x, xs.at[0], xsem.at[0]).start()
         pl.semaphore_wait(bar, n - 1)
         step = T // 2
         own = [x.at[pl.ds(h * step, step)] for h in range(2)]
-        for axis in range(2):
+        def spread(axis):
             for h in range(2):
                 for d in NEAR:
                     relay(h, HERE, axis, d, None, own[h])
+
+        spread(0)
+
+        for e in range(el):
+            for cp in wcopies(e):
+                cp.start()
+        pltpu.make_async_copy(x, xs.at[0], xsem.at[0]).wait()
+        for i, table in enumerate(_tables(xs[0], wr[...], idx[...], C)):
+            flat[:, :C] = table
+            wide = jnp.concatenate([flat[pl.ds(e, n, stride=el), :][:, :C] for e in range(el)], axis=1)
+            for m in range(n):
+                pk[i, m // X, m % X] = wide[m:m + 1]
+        tab_in[me] = pk[0, mo, mx]
+        pk_a[mo] = pk[:, mo]
+        pk_b[mc] = pk[:, :, pl.ds(2 * mc, 2)]
         for h in range(2):
             share(h, HERE, own[h])
 
@@ -258,25 +284,16 @@
             return 0
 
         lax.fori_loop(1, n, tell, 0)
-        pltpu.make_async_copy(pk.at[0, mo, mx], tab_in.at[me], tsem2.at[0, 0]).start()
-        for d in range(4):
-            yo, xo = lax.rem(mo + d, O), lax.rem(mc + d, W)
-            if d == 0:
-                pltpu.make_async_copy(pk.at[:, mo], pk_a.at[mo], tsem2.at[1, 0]).start()
-                pltpu.make_async_copy(pk.at[:, :, pl.ds(2 * mc, 2)], pk_b.at[mc], tsem2.at[2, 0]).start()
-            else:
-                tsend(0, d).start()
-                tsend(1, d).start()
-        for e in range(el):
-            for cp in wcopies(e):
-                cp.start()
+        for d in range(1, O):
+            for v in range(2):
+                tsend(v, d).start()
+        spread(1)
         tok = lax.broadcasted_iota(jnp.int32, (T, B), 0).astype(F32)
 
         for axis in range(2):
             for h in range(2):
                 for d in NEAR:
                     event(h, (0, d) if axis else (d, 0))
-        pltpu.make_async_copy(pk.at[0, mo, mx], tab_in.at[me], tsem2.at[0, 0]).wait()
         allrows = pltpu.make_async_remote_copy(
             src_ref=tab_in.at[pl.ds(0, n - 1)], dst_ref=tab_in.at[pl.ds(0, n - 1)], send_sem=tsem.at[0],
             recv_sem=tsem.at[1], device_id=other(), device_id_type=MESH)
@@ -384,8 +401,6 @@
     pl.run_scoped(experts, pltpu.VMEM((el, D, FF), BF16), pltpu.VMEM((el, D, FF), BF16),
                   pltpu.VMEM((el, FF, D), BF16), pltpu.VMEM((el, half, D), BF16))
 
-    pltpu.make_async_copy(pk.at[:, mo], pk_a.at[mo], tsem2.at[1, 0]).wait()
-    pltpu.make_async_copy(pk.at[:, :, pl.ds(2 * mc, 2)], pk_b.at[mc], tsem2.at[2, 0]).wait()
     for d in range(1, 4):
         tsend(0, d).wait()
         tsend(1, d).wait()
@@ -458,10 +473,7 @@
             rows = [ref[(d, 0) + r0(c)] for c in range(2)]
             gs = [ref[(d, 1) + r0(c)] for c in range(2)]
             w = jnp.where(tokf == jnp.concatenate(rows, axis=1), jnp.concatenate(gs, axis=1), 0.0)
-            hi = w.astype(BF16)
-            r = w - hi.astype(F32)
-            mid = r.astype(BF16)
-            return hi, mid, (r - mid.astype(F32)).astype(BF16)
+            return _split(w)
 
         def comb(p, _):
             slot = lax.rem(p, 2)
@@ -569,10 +581,8 @@
         el, _, FF = w1.shape
         C = 2 * T * k // E
         B = el * C
-        g = _gate(x, wr, idx)
-        tab, gs = _tables(idx, g, E, C)
-        pk = jnp.stack((tab.astype(F32), gs)).reshape(2, O, X, 1, B)
         anyspec = pl.BlockSpec(memory_space=pl.ANY)
+        vspec = pl.BlockSpec(memory_space=pltpu.VMEM)
         y = pl.pallas_call(
             functools.partial(_kernel, O, X, el, C),
             out_shape=(jax.ShapeDtypeStruct((T, D), BF16),
@@ -580,11 +590,13 @@
                        jax.ShapeDtypeStruct((2, n * B, D // 2), BF16),
                        jax.ShapeDtypeStruct((2, n * B, D // 2), BF16),
                        jax.ShapeDtypeStruct((2, 2, T, D // 2), F32)),
-            in_specs=[anyspec] * 5,
+            in_specs=[anyspec, vspec, vspec, anyspec, anyspec, anyspec],
             out_specs=(anyspec,) * 5,
             scratch_shapes=[
                 pltpu.VMEM((2, T, D), BF16),
                 pltpu.VMEM((2, 4 * C, D), BF16),
+                pltpu.VMEM((2, O, X, 1, B), F32),
+                pltpu.VMEM((E, E), F32),
                 pltpu.VMEM((n, 1, B), F32),
                 pltpu.VMEM((O, 2, X, 1, B), F32),
                 pltpu.VMEM((X // 2, 2, O, 2, 1, B), F32),
@@ -608,7 +620,7 @@
             ],
             compiler_params=pltpu.CompilerParams(
                 collective_id=0, has_side_effects=True, vmem_limit_bytes=67043328),
-        )(x, pk, w1, w3, w2)
+        )(x, wr, idx, w1, w3, w2)
         return y[0]
 
     return jax.shard_map(local, mesh=mesh, in_specs=(tok, P(None, None), tok, wsp, wsp, wsp), out_specs=tok, check_vma=False)

time: 448 us -> 443 us (0.989)
  no operation moved by 1% of the time
where the time goes in v5:
time: 443 us; the launch traced here: 442 us
  Pallas kernels  438 us (99%)
  local copies, waits for them, and re-layouts  4.71 us (1%)
    pallas_call x1, Pallas kernels, local(): pl.pallas_call(functools.partial(_kernel, O, X, el, C), out_shape=(jax.Sh...  438 us

profile of v5, /device:TPU:97, one launch (start us, length us, event | category | flops | bytes accessed | tf_op | source)
XLA Modules:
  0.0 442.4 jit_solution(70106819103054651)
XLA Ops:
  0.0 1.6 copy.7.idx
  1.6 437.7 %shard_map.64 = (bf16[512,2048]{1,0:T(8,128)(2,1)}, bf16[16384,2048]{1,0:T(8,128)(2,1)}, bf16[2,8192,1024]{2,1,0:T(8,128)(2,1)}, bf16[2,8192,1024]{2,1,0:T(8,128)(2,1)}, f32[2,2,512,1024]{3,2,1,0:T(8,128)}) custom-call(bf16[512,2048]{1,0:T(8,128)(2,1)} %x.1, bf16[2048,128]{1,0:T(8,128)(2,1)} %wr.1, s32[512,8]{1,0:T(8,128)} %copy.7.idx, ...), custom_call_target="tpu_custom_call" | custom-call | tf_op jit(solution)/shard_map/pallas_call | solution.py:586
  439.2 3.2 copy.9

commit v6 on v5

--- a/solution.py
+++ b/solution.py
@@ -54,12 +54,12 @@
     return tab, (res[1][:, :C] + res[1][:, C:2 * C]) + res[2][:, :C]
 
 
-ORDER = ((0, 1), (0, 3), (1, 0), (3, 0), (0, 0), (0, 2), (1, 1), (3, 3),
-         (1, 3), (3, 1), (1, 2), (3, 2), (2, 1), (2, 3), (2, 0), (2, 2))
+ORDER = ((0, 1), (0, 3), (1, 0), (3, 0), (2, 0), (0, 2), (1, 1), (3, 3),
+         (1, 3), (3, 1), (1, 2), (3, 2), (2, 1), (2, 3), (0, 0), (2, 2))
 NEAR = (1, 3)
 EARLY, MID, LATE = range(3)
 HERE = (0, 0)
-TIMES = (0, 3, 5, 6, 8, 9, 12, 13, 15, 16, 20)
+TIMES = (0, 1, 3, 4, 5, 6, 8, 9, 10, 11, 22)
 
 
 def _lut(vals, i):

time: 443 us -> 443 us (level)
  no operation moved by 1% of the time
where the time goes in v6:
time: 443 us; the launch traced here: 442 us
  Pallas kernels  438 us (99%)
  local copies, waits for them, and re-layouts  4.71 us (1%)
    pallas_call x1, Pallas kernels, local(): pl.pallas_call(functools.partial(_kernel, O, X, el, C), out_shape=(jax.Sh...  438 us

profile of v6, /device:TPU:97, one launch (start us, length us, event | category | flops | bytes accessed | tf_op | source)
XLA Modules:
  0.0 442.5 jit_solution(6029148910594669322)
XLA Ops:
  0.0 1.6 copy.7.idx
  1.6 437.7 %shard_map.64 = (bf16[512,2048]{1,0:T(8,128)(2,1)}, bf16[16384,2048]{1,0:T(8,128)(2,1)}, bf16[2,8192,1024]{2,1,0:T(8,128)(2,1)}, bf16[2,8192,1024]{2,1,0:T(8,128)(2,1)}, f32[2,2,512,1024]{3,2,1,0:T(8,128)}) custom-call(bf16[512,2048]{1,0:T(8,128)(2,1)} %x.1, bf16[2048,128]{1,0:T(8,128)(2,1)} %wr.1, s32[512,8]{1,0:T(8,128)} %copy.7.idx, ...), custom_call_target="tpu_custom_call" | custom-call | tf_op jit(solution)/shard_map/pallas_call | solution.py:586
  439.3 3.2 copy.9
